TPU v7x, 32 devices: a 4x2x2 block of a 4x4x8 slice. The times are simulated.
32 devices in a mesh: dp: 4 (over y, z), ep: 8 (over x, core).
Axes of the slice: x: 4, y: 2, z: 2, core: 2. Of those that a mesh axis runs over, the one named last changes fastest.
The devices are a block of a 4x4x8 slice.
Arguments:
- hidden: bfloat16 [4096, 4096], P(('dp', 'ep')), parts along dimension 0
- k_cache: bfloat16 [4096, 32, 8, 128], P(('dp', 'ep')), parts along dimension 0
- v_cache: bfloat16 [4096, 32, 8, 128], P(('dp', 'ep')), parts along dimension 0
- seq_lens: int32 [4096], P(('dp', 'ep')), parts along dimension 0
- expert_ids: int32 [4096, 2], P(('dp', 'ep')), parts along dimension 0
- attn_gain: bfloat16 [4096], replicated
- w_query: bfloat16 [4096, 4096], replicated
- w_key: bfloat16 [4096, 1024], replicated
- w_value: bfloat16 [4096, 1024], replicated
- w_out: bfloat16 [4096, 4096], replicated
- ffn_gain: bfloat16 [4096], replicated
- w_router: bfloat16 [4096, 16], replicated
- w_gate: bfloat16 [16, 4096, 960], P('ep')
- w_up: bfloat16 [16, 4096, 960], P('ep')
- w_down: bfloat16 [16, 960, 4096], P('ep')
Outputs:
- output 1: bfloat16 [4096, 4096], P(('dp', 'ep')), parts along dimension 0
- output 2: bfloat16 [4096, 32, 8, 128], P(('dp', 'ep')), parts along dimension 0
- output 3: bfloat16 [4096, 32, 8, 128], P(('dp', 'ep')), parts along dimension 0
There are 4 independent parts. A program takes and returns all parts, laid end to end along the dimension named above; an argument that names none is the same for every part.
All inputs are finite; a program needn't handle non-finite values.
Results may differ from a plain program's by a relative error of at most 0.0149361.
Values are sent between devices in bfloat16 or wider.
A program may use at most 768 MiB of HBM per device.

v0:
```python
import jax
import jax.numpy as jnp
from jax import lax
from jax.sharding import PartitionSpec as P

NORM_EPS = 1e-5
ROPE_THETA = 1000000.0


def rms_scale(row_block, gain_vec):
    rows_f32 = row_block.astype(jnp.float32)
    inv_rms = lax.rsqrt(jnp.mean(rows_f32 * rows_f32, axis=-1, keepdims=True) + NORM_EPS)
    return (rows_f32 * inv_rms * gain_vec.astype(jnp.float32)).astype(jnp.bfloat16)


def rope_rotate(vectors, positions):
    half_dim = vectors.shape[-1] // 2
    inv_freq = ROPE_THETA ** (-2.0 * jnp.arange(half_dim, dtype=jnp.float32) / vectors.shape[-1])
    angles = positions.astype(jnp.float32)[:, None, None] * inv_freq
    cosines = jnp.cos(angles)
    sine_vals = jnp.sin(angles)
    vec_f32 = vectors.astype(jnp.float32)
    low_half = vec_f32[..., :half_dim]
    high_half = vec_f32[..., half_dim:]
    return jnp.concatenate([low_half * cosines - high_half * sine_vals, high_half * cosines + low_half * sine_vals], axis=-1).astype(jnp.bfloat16)


def attention_block(hidden, k_cache, v_cache, seq_lens, attn_gain, w_query, w_key, w_value, w_out):
    tokens, seq_len, kv_heads, head_dim = k_cache.shape
    q_heads = w_query.shape[1] // head_dim
    groups = q_heads // kv_heads
    normed = rms_scale(hidden, attn_gain)
    q_proj = jnp.dot(normed, w_query, preferred_element_type=jnp.float32).astype(jnp.bfloat16)
    q_proj = rope_rotate(q_proj.reshape(tokens, q_heads, head_dim), seq_lens).reshape(tokens, kv_heads, groups, head_dim)
    key_new = jnp.dot(normed, w_key, preferred_element_type=jnp.float32).astype(jnp.bfloat16)
    key_new = rope_rotate(key_new.reshape(tokens, kv_heads, head_dim), seq_lens)
    value_new = jnp.dot(normed, w_value, preferred_element_type=jnp.float32).astype(jnp.bfloat16).reshape(tokens, kv_heads, head_dim)
    positions = jnp.arange(seq_len)
    slot_hit = (positions[None, :] == seq_lens[:, None])[:, :, None, None]
    k_cache_new = jnp.where(slot_hit, key_new[:, None], k_cache)
    v_cache_new = jnp.where(slot_hit, value_new[:, None], v_cache)
    scores = jnp.einsum('tkgh,tskh->tkgs', q_proj, k_cache_new, preferred_element_type=jnp.float32) * head_dim ** -0.5
    visible = (positions[None, :] <= seq_lens[:, None])[:, None, None, :]
    attn_probs = jax.nn.softmax(jnp.where(visible, scores, -jnp.inf), axis=-1).astype(jnp.bfloat16)
    attn_mix = jnp.einsum('tkgs,tskh->tkgh', attn_probs, v_cache_new, preferred_element_type=jnp.float32).astype(jnp.bfloat16)
    attn_out = jnp.dot(attn_mix.reshape(tokens, q_heads * head_dim), w_out, preferred_element_type=jnp.float32)
    resid_out = (hidden.astype(jnp.float32) + attn_out).astype(jnp.bfloat16)
    return resid_out, k_cache_new, v_cache_new


def ffn_gates(resid_out, ffn_gain, w_router, expert_ids):
    normed_ffn = rms_scale(resid_out, ffn_gain)
    logits = jnp.dot(normed_ffn, w_router, preferred_element_type=jnp.float32)
    chosen = expert_ids[:, :, None] == jnp.arange(w_router.shape[1])
    picked = jnp.sum(jnp.where(chosen, logits[:, None, :], 0.0), axis=-1)
    return normed_ffn, jax.nn.softmax(picked, axis=-1)


def choice_slots(expert_ids, expert_list, cap_slots):
    hit_mask = expert_ids[..., None] == expert_list
    hit_counts = hit_mask.reshape(hit_mask.shape[:-3] + (-1, hit_mask.shape[-1])).astype(jnp.int32)
    before = (jnp.cumsum(hit_counts, axis=-2) - hit_counts).reshape(hit_mask.shape)
    return (hit_mask[..., None] & (before[..., None] == jnp.arange(cap_slots))).astype(jnp.bfloat16)


def solution(mesh):
    n_ep = mesh.shape['ep']
    row_spec = P(('dp', 'ep'), None)
    cache_spec = P(('dp', 'ep'), None, None, None)
    expert_spec = P('ep', None, None)
    in_specs = (row_spec, cache_spec, cache_spec, P(('dp', 'ep')), row_spec, P(), P(), P(), P(), P(), P(), P(), expert_spec, expert_spec, expert_spec)
    out_specs = (row_spec, cache_spec, cache_spec)

    def device_step(hidden, k_cache, v_cache, seq_lens, expert_ids, attn_gain, w_query, w_key, w_value, w_out, ffn_gain, w_router, w_gate, w_up, w_down):
        tokens, d_model = hidden.shape
        local_experts = w_gate.shape[0]
        n_experts = local_experts * n_ep
        cap_slots = 4 * tokens // n_experts
        resid_out, k_cache_new, v_cache_new = attention_block(hidden, k_cache, v_cache, seq_lens, attn_gain, w_query, w_key, w_value, w_out)
        normed_ffn, gates = ffn_gates(resid_out, ffn_gain, w_router, expert_ids)
        slot_sel = choice_slots(expert_ids, jnp.arange(n_experts), cap_slots)
        send_buf = jnp.einsum('tkec,td->ecd', slot_sel, normed_ffn, preferred_element_type=jnp.float32).astype(jnp.bfloat16)
        send_buf = send_buf.reshape(n_ep, local_experts, cap_slots, d_model)
        recv_buf = lax.all_to_all(send_buf, 'ep', 0, 0, tiled=True)
        gate_act = jnp.einsum('sxcd,xdf->sxcf', recv_buf, w_gate, preferred_element_type=jnp.float32)
        up_act = jnp.einsum('sxcd,xdf->sxcf', recv_buf, w_up, preferred_element_type=jnp.float32)
        inner_act = (jax.nn.silu(gate_act) * up_act).astype(jnp.bfloat16)
        expert_out = jnp.einsum('sxcf,xfd->sxcd', inner_act, w_down, preferred_element_type=jnp.float32).astype(jnp.bfloat16)
        returned = lax.all_to_all(expert_out, 'ep', 0, 0, tiled=True).reshape(n_experts, cap_slots, d_model)
        routed = jnp.einsum('tkec,ecd->tkd', slot_sel, returned, preferred_element_type=jnp.float32)
        out_f32 = resid_out.astype(jnp.float32) + jnp.sum(gates[:, :, None] * routed, axis=1)
        return out_f32.astype(jnp.bfloat16), k_cache_new, v_cache_new

    return jax.shard_map(device_step, mesh=mesh, in_specs=in_specs, out_specs=out_specs, check_vma=False)
```

profile of v0, /device:TPU:81, one launch (start us, length us, event | category | flops | bytes accessed | tf_op | source)
XLA Modules:
  0.0 232.5 jit_solution(733030926345850233)
XLA Ops:
  0.6 0.0 copy-start
  0.7 0.7 convert_element_type.95
  1.4 0.7 iota_compare_fusion.2
  2.1 0.7 iota_compare_fusion.5
  2.8 0.8 copy.32
  3.6 0.1 eq.79
  3.7 0.1 eq.75
  3.9 1.5 fusion.23
  5.4 0.7 convert_element_type.90
  6.1 0.7 convert_element_type.104
  6.8 0.6 reduce-window.6
  7.4 0.2 slice_reduce_fusion
  7.6 0.1 fusion.56
  7.7 0.1 copy.35
  7.8 0.1 copy.36
  7.9 0.0 copy-start.1
  7.9 5.1 %fusion.42 = bf16[16,8,8,128]{3,1,2,0:T(8,128)(2,1)S(1)} fusion(bf16[4096,1024]{1,0:T(8,128)(2,1)} %param.23, bf16[128,4096]{1,0:T(8,128)(2,1)} %param.15, f32[4096]{0:T(1024)S(1)} %convert_element_type.90, f32[128]{0:T(128)S(1)} %add_rsqrt_fusion.1), kind=kOutput, calls=%fused_computation.53 | convolution fusion | flops 1075970048 | bytes 9716224 | tf_op jit(solution)/shard_map/dot_general | solution.py:37
  13.0 0.0 copy-done.1
  13.0 4.7 %fusion.41 = f32[16,8,8,128]{3,1,2,0:T(8,128)S(1)} fusion(bf16[4096,1024]{1,0:T(8,128)(2,1)} %param.22, bf16[128,4096]{1,0:T(8,128)(2,1)S(1)} %copy-done.1, f32[4096]{0:T(1024)S(1)} %convert_element_type.90, f32[128]{0:T(128)S(1)} %add_rsqrt_fusion.1), kind=kOutput, calls=%fused_computation.52 | convolution fusion | flops 1076101120 | bytes 9978368 | tf_op jit(solution)/shard_map/dot_general | solution.py:35
  17.7 0.1 copy.46
  17.8 13.0 %fusion.31 = f32[16,8,32,128]{3,1,2,0:T(8,128)S(1)} fusion(bf16[4096,4096]{1,0:T(8,128)(2,1)} %param.21, bf16[128,4096]{1,0:T(8,128)(2,1)S(1)} %copy-done.1, f32[4096]{0:T(1024)S(1)} %convert_element_type.90, f32[128]{0:T(128)S(1)} %add_rsqrt_fusion.1), kind=kOutput, calls=%fused_computation.46 | convolution fusion | flops 4298113024 | bytes 36717056 | tf_op jit(solution)/shard_map/dot_general | solution.py:33
  30.8 0.4 copy.45
  31.2 0.3 multiply_cosine_fusion
  31.5 0.3 subtract_convert_fusion.1
  31.8 0.9 subtract_convert_fusion
  32.7 0.1 pad_maximum_fusion
  32.9 11.9 %broadcast_select_fusion.1 = (bf16[128,32,8,128]{3,2,1,0:T(8,128)(2,1)}, bf16[128,32,8,128]{3,2,1,0:T(8,128)(2,1)}) fusion(bf16[128,32,8,128]{3,2,1,0:T(8,128)(2,1)} %param.16, pred[128,32]{1,0:T(8,128)(4,1)S(1)} %get-tuple-element.12, bf16[128,8,128]{2,1,0:T(8,128)(2,1)S(1)} %pad_maximum_fusion, bf16[128,32,8,128]{3,2,1,0:T(8,128)(2,1)} %param.17, ...), kind=kLoop, calls=%fused_computation.12 | loop fusion | flops 8388608 | bytes 34082816 | tf_op jit(solution)/shard_map/jit(_where)/select_n | solution.py:40
  44.7 9.4 %fusion.67 = (f32[128,8,4]{2,1,0:T(8,128)}, f32[128,8,4,32]{3,2,1,0:T(4,128)}) fusion(pred[128,32]{1,0:T(8,128)(4,1)S(1)} %get-tuple-element.11, bf16[128,32,8,128]{3,2,1,0:T(8,128)(2,1)} %get-tuple-element.7, bf16[128,8,4,64]{3,2,1,0:T(4,128)(2,1)S(1)} %bitcast.91, bf16[128,8,4,64]{3,2,1,0:T(4,128)(2,1)S(1)} %bitcast.90), kind=kOutput, calls=%fused_computation.94 | convolution fusion | flops 36175904 | bytes 9981952 | tf_op jit(solution)/shard_map/sub | solution.py:44
  54.1 6.5 %fusion.37 = bf16[128,8,4,128]{3,2,1,0:T(4,128)(2,1)S(1)} fusion(bf16[128,32,8,128]{3,2,1,0:T(8,128)(2,1)} %get-tuple-element.8, f32[128,8,4,32]{3,2,1,0:T(4,128)} %get-tuple-element.14, f32[128,8,4]{2,1,0:T(8,128)} %get-tuple-element.13), kind=kOutput, calls=%fused_computation.48 | convolution fusion | flops 34340864 | bytes 9977856 | tf_op jit(solution)/shard_map/tkgs,tskh->tkgh/dot_general | solution.py:45
  60.6 1.6 reshape.214
  62.3 13.3 %multiply_reduce_fusion = (f32[128]{0:T(128)S(1)}, f32[128,4096]{1,0:T(8,128)S(1)}) fusion(bf16[128,4096]{1,0:T(8,128)(2,1)} %reshape.214, bf16[4096,4096]{1,0:T(8,128)(2,1)} %param.24, bf16[128,4096]{1,0:T(8,128)(2,1)S(1)} %copy-done.1), kind=kOutput, calls=%fused_computation.39 | convolution fusion | flops 4298113024 | bytes 37749248 | tf_op jit(solution)/shard_map/dot_general | solution.py:46
  75.6 0.1 convert_reduce_fusion
  75.7 1.3 convolution_convert_fusion
  77.1 54.4 %all_to_all.10 = bf16[8,2,32,4096]{3,2,1,0:T(8,128)(2,1)} all-to-all(bf16[8,2,32,4096]{3,2,1,0:T(8,128)(2,1)S(1)} %bitcast.87), channel_id=1, replica_groups=mesh['dp'=4,'ep'=8] {'ep'}, dimensions={0} | all-to-all | bytes 8388608 | tf_op jit(solution)/shard_map/all_to_all | solution.py:84
  131.5 12.6 %fusion.5 = f32[2,8,32,960]{3,2,1,0:T(8,128)} fusion(bf16[2,4096,960]{1,2,0:T(8,128)(2,1)} %param.27, bf16[8,2,32,4096]{3,2,1,0:T(8,128)(2,1)} %all_to_all.10), kind=kOutput, calls=%fused_computation.5 | convolution fusion | flops 4026531840 | bytes 21889024 | tf_op jit(solution)/shard_map/sxcd,xdf->sxcf/dot_general | solution.py:85
  144.1 16.6 %fusion.26 = bf16[8,2,32,960]{3,2,0,1:T(8,128)(2,1)S(1)} fusion(f32[2,8,32,960]{3,2,1,0:T(8,128)} %fusion.5, bf16[2,4096,960]{1,2,0:T(8,128)(2,1)} %param.28, bf16[8,2,32,4096]{3,2,1,0:T(8,128)(2,1)} %all_to_all.10), kind=kOutput, calls=%fused_computation.31 | convolution fusion | flops 4029480960 | bytes 22872064 | tf_op jit(solution)/shard_map/sxcd,xdf->sxcf/dot_general | solution.py:86
  160.7 10.2 %fusion.14 = bf16[8,2,32,4096]{3,2,0,1:T(8,128)(2,1)S(1)} fusion(bf16[8,2,32,960]{3,2,0,1:T(8,128)(2,1)S(1)} %fusion.26, bf16[2,960,4096]{2,1,0:T(8,128)(2,1)} %param.29), kind=kOutput, calls=%fused_computation.15 | convolution fusion | flops 4028628992 | bytes 20905984 | tf_op jit(solution)/shard_map/sxcf,xfd->sxcd/dot_general | solution.py:88
  170.9 2.2 copy.39
  173.2 5.6 %all-to-all-start.1 = ((bf16[8,2,32,4096]{3,2,1,0:T(8,128)(2,1)}), bf16[8,2,32,4096]{3,2,1,0:T(8,128)(2,1)}, u32[]{:S(2)}, u32[]{:S(2)}) async-start(bf16[8,2,32,4096]{3,2,1,0:T(8,128)(2,1)} %copy.39), calls=%async_computation.1 | async-start | bytes 8388608 | tf_op jit(solution)/shard_map/all_to_all | solution.py:89
  178.7 0.0 copy-done
  178.7 0.0 copy-start.2
  178.7 0.4 fusion.63
  179.2 0.2 copy-done.2
  179.5 47.9 %all-to-all-done.1 = bf16[8,2,32,4096]{3,2,1,0:T(8,128)(2,1)} async-done(((bf16[8,2,32,4096]{3,2,1,0:T(8,128)(2,1)}), bf16[8,2,32,4096]{3,2,1,0:T(8,128)(2,1)}, u32[]{:S(2)}, u32[]{:S(2)}) %all-to-all-start.1) | async-done | bytes 4194336 | tf_op jit(solution)/shard_map/all_to_all | solution.py:89
  227.4 3.9 %fusion.30 = f32[128,4096]{1,0:T(8,128)S(1)} fusion(bf16[16,32,4096,1]{2,1,0,3:T(8,128)(2,1)} %bitcast.16, f32[128,2]{0,1:T(2,128)S(1)} %fusion.58, s32[128,2,16]{0,2,1:T(8,128)S(1)} %copy.36, pred[128,2,16]{0,2,1:T(8,128)(4,1)S(1)} %iota_compare_fusion.5), kind=kOutput, calls=%fused_computation.45 | convolution fusion | flops 1075576832 | bytes 6312960 | tf_op jit(solution)/shard_map/tkec,ecd->tkd/dot_general | solution.py:90
  231.3 1.2 add_convert_fusion
  (11 shorter events, 0.2 us)
Async XLA Ops:
  0.6 178.1 %copy-start = (bf16[4096,16]{0,1:T(8,128)(2,1)S(1)}, bf16[4096,16]{0,1:T(8,128)(2,1)}, u32[]{:S(2)}) copy-start(bf16[4096,16]{0,1:T(8,128)(2,1)} %param.26) | copy-start | bytes 393220
  7.9 5.2 %copy-start.1 = (bf16[128,4096]{1,0:T(8,128)(2,1)S(1)}, bf16[128,4096]{1,0:T(8,128)(2,1)}, u32[]{:S(2)}) copy-start(bf16[128,4096]{1,0:T(8,128)(2,1)} %param.15) | copy-start | bytes 3145732
  173.2 54.2 %all-to-all-start.1 = ((bf16[8,2,32,4096]{3,2,1,0:T(8,128)(2,1)}), bf16[8,2,32,4096]{3,2,1,0:T(8,128)(2,1)}, u32[]{:S(2)}, u32[]{:S(2)}) async-start(bf16[8,2,32,4096]{3,2,1,0:T(8,128)(2,1)} %copy.39), calls=%async_computation.1 | async-start | bytes 8388608 | tf_op jit(solution)/shard_map/all_to_all | solution.py:89
  178.7 0.7 copy-start.2
where the time goes:
time: 233 us
  matrix products  97.1 us (42%)
  blocking collectives  54.4 us (23%)
  waiting for transfers between devices  47.9 us (21%)
  other arithmetic  20.7 us (9%)
  local copies, waits for them, and re-layouts  6.02 us (3%)
  starting transfers between devices  5.55 us (2%)
    all_to_all x1, blocking collectives, device_step(): recv_buf = lax.all_to_all(send_buf, 'ep', 0, 0, tiled=True)  54.4 us
    all_to_all x1, waiting for transfers between devices, device_step(): lax.all_to_all(expert_out, 'ep', 0, 0, tiled=True)  47.9 us
    dot_general x1, matrix products, device_step(): jnp.einsum('sxcd,xdf->sxcf', recv_buf, w_up, preferred_element_type=jnp.f...  16.6 us
    dot_general x1, matrix products, attention_block(): jnp.dot(attn_mix.reshape(tokens, q_heads * head_dim), w_out, preferred_el...  13.3 us
    dot_general x1, matrix products, attention_block(): jnp.dot(normed, w_query, preferred_element_type=jnp.float32)  13 us
    dot_general x1, matrix products, device_step(): jnp.einsum('sxcd,xdf->sxcf', recv_buf, w_gate, preferred_element_type=jnp...  12.6 us
    select_n x1, other arithmetic, attention_block(): k_cache_new = jnp.where(slot_hit, key_new[:, None], k_cache)  11.9 us
    dot_general x1, matrix products, device_step(): jnp.einsum('sxcf,xfd->sxcd', inner_act, w_down, preferred_element_type=jn...  10.2 us
  transfers between devices with their start and end apart: 1, of which 1 were waited for; matrix products, arithmetic and copies ran while one was open for 0% of the time, Pallas kernels for 0%

commit v1 on v0

v1 whole, which is shorter than its diff:
```python
import functools

import jax
import jax.numpy as jnp
import numpy as np
from jax import lax
from jax.experimental import pallas as pl
from jax.experimental.pallas import tpu as pltpu
from jax.sharding import PartitionSpec as P

NORM_EPS = 1e-5
ROPE_THETA = 1000000.0
VMEM_LIMIT = 67000000


def spread_gain(gain, gains):
    lanes = gain.shape[1]
    wide = gain[...].astype(jnp.float32)
    for r in range(gain.shape[0]):
        gains[:, r * lanes:(r + 1) * lanes] = wide[r:r + 1, :]


def column_of(row):
    return jnp.broadcast_to(row, (row.shape[1], row.shape[1])).T


def attn_kernel(
    lens, hidden, gain, lens_row, freq, wq, wk, wv, kc, vc,
    mix, kn, vn,
    normed, wbuf, kbuf, vbuf, heads, mixed, cos, sin, gains, wsem, ksem, vsem, kout, vout,
    *, kv_heads, tile, chunk,
):
    tokens, d_model = hidden.shape
    seq_len, head_dim = kc.shape[1], kc.shape[3]
    q_tiles, kv_tiles = wq.shape[1] // tile, wk.shape[1] // tile
    n_tiles = q_tiles + 2 * kv_tiles
    per_tile = tile // head_dim
    q_heads = wq.shape[1] // head_dim
    groups = q_heads // kv_heads
    pitch = tokens + 8
    slots = wbuf.shape[0]
    n_chunks = tokens // chunk

    def fetch(i, slot):
        @pl.when(i < q_tiles)
        def _():
            pltpu.make_async_copy(wq.at[:, pl.ds(pl.multiple_of(i * tile, tile), tile)], wbuf.at[slot], wsem.at[slot]).start()

        @pl.when(jnp.logical_and(i >= q_tiles, i < q_tiles + kv_tiles))
        def _():
            pltpu.make_async_copy(wk.at[:, pl.ds(pl.multiple_of((i - q_tiles) * tile, tile), tile)], wbuf.at[slot], wsem.at[slot]).start()

        @pl.when(jnp.logical_and(i >= q_tiles + kv_tiles, i < n_tiles))
        def _():
            pltpu.make_async_copy(wv.at[:, pl.ds(pl.multiple_of((i - q_tiles - kv_tiles) * tile, tile), tile)], wbuf.at[slot], wsem.at[slot]).start()

    def rows(c):
        return pl.ds(pl.multiple_of(c * chunk, chunk), chunk)

    for i in range(slots):
        fetch(jnp.int32(i), i)

    spread_gain(gain, gains)
    x = hidden[...].astype(jnp.float32)
    inv = lax.rsqrt(jnp.mean(x * x, axis=-1, keepdims=True) + NORM_EPS)
    normed[...] = (x * inv * gains[...]).astype(jnp.bfloat16)
    angles = column_of(lens_row[...].astype(jnp.float32)) * freq[...]
    sines = jnp.sin(angles)
    lane = lax.broadcasted_iota(jnp.int32, angles.shape, 1)
    cos[...] = jnp.cos(angles)
    sin[...] = jnp.where(lane < head_dim // 2, -sines, sines)

    def project(i, carry):
        slot = lax.rem(i, slots)
        pltpu.make_async_copy(wq.at[:, pl.ds(0, tile)], wbuf.at[slot], wsem.at[slot]).wait()
        out = jnp.dot(normed[...], wbuf[slot], preferred_element_type=jnp.float32)
        fetch(i + slots, slot)

        @pl.when(i + slots == n_tiles)
        def _():
            def start(c, carry):
                pltpu.make_async_copy(kc.at[rows(c)], kbuf.at[rows(c)], ksem.at[c]).start()
                pltpu.make_async_copy(vc.at[rows(c)], vbuf.at[rows(c)], vsem.at[c]).start()
                return carry

            lax.fori_loop(0, n_chunks, start, 0)

        turn = i < q_tiles + kv_tiles
        c_val = jnp.where(turn, cos[...], 1.0)
        s_val = jnp.where(turn, sin[...], 0.0)
        for j in range(per_tile):
            block = out[:, j * head_dim:(j + 1) * head_dim].astype(jnp.bfloat16).astype(jnp.float32)
            block = block * c_val + pltpu.roll(block, head_dim // 2, axis=1) * s_val
            block = block.astype(jnp.bfloat16).astype(jnp.float32)
            heads[pl.ds(pl.multiple_of((i * per_tile + j) * pitch, 8), tokens), :] = block
        return carry

    lax.fori_loop(0, n_tiles, project, 0)

    head_of = lax.broadcasted_iota(jnp.int32, (q_heads, seq_len * kv_heads), 0) // groups
    column = lax.broadcasted_iota(jnp.int32, (q_heads, seq_len * kv_heads), 1)
    own = head_of == lax.rem(column, kv_heads)

    def attend(c, carry):
        pltpu.make_async_copy(kc.at[rows(c)], kbuf.at[rows(c)], ksem.at[c]).wait()
        pltpu.make_async_copy(vc.at[rows(c)], vbuf.at[rows(c)], vsem.at[c]).wait()
        base = c * chunk
        for j in range(chunk):
            t = base + j
            n = lens[t]
            kbuf[t, n] = heads[pl.ds(q_heads * pitch + t, kv_heads, stride=pitch), :].astype(jnp.bfloat16)
            vbuf[t, n] = heads[pl.ds((q_heads + kv_heads) * pitch + t, kv_heads, stride=pitch), :].astype(jnp.bfloat16)
        probs = []
        for j in range(chunk):
            t = base + j
            q = heads[pl.ds(t, q_heads, stride=pitch), :].astype(jnp.bfloat16)
            keys = kbuf[t].reshape(seq_len * kv_heads, head_dim)
            score = lax.dot_general(q, keys, (((1,), (1,)), ((), ())), preferred_element_type=jnp.float32)
            score = score * head_dim ** -0.5
            seen = jnp.logical_and(own, column < (lens[t] + 1) * kv_heads)
            score = jnp.where(seen, score, -jnp.inf)
            e = jnp.exp(score - jnp.max(score, axis=-1, keepdims=True))
            probs.append((e / jnp.sum(e, axis=-1, keepdims=True)).astype(jnp.bfloat16))
        for j in range(chunk):
            t = base + j
            values = vbuf[t].reshape(seq_len * kv_heads, head_dim)
            o = jnp.dot(probs[j], values, preferred_element_type=jnp.float32)
            mixed[pl.ds(t, q_heads, stride=pitch), :] = o
        pltpu.make_async_copy(kbuf.at[rows(c)], kn.at[rows(c)], kout.at[c]).start()
        pltpu.make_async_copy(vbuf.at[rows(c)], vn.at[rows(c)], vout.at[c]).start()
        return carry

    lax.fori_loop(0, n_chunks, attend, 0)

    for h in range(q_heads):
        mix[:, h * head_dim:(h + 1) * head_dim] = mixed[h * pitch:h * pitch + tokens, :].astype(jnp.bfloat16)

    def drain(c, carry):
        pltpu.make_async_copy(kbuf.at[rows(c)], kn.at[rows(c)], kout.at[c]).wait()
        pltpu.make_async_copy(vbuf.at[rows(c)], vn.at[rows(c)], vout.at[c]).wait()
        return carry

    lax.fori_loop(0, n_chunks, drain, 0)


def attention(hidden, k_cache, v_cache, seq_lens, attn_gain, w_query, w_key, w_value):
    tokens, seq_len, kv_heads, head_dim = k_cache.shape
    d_model = hidden.shape[1]
    n_heads = w_query.shape[1] // head_dim
    all_heads = n_heads + 2 * kv_heads
    half = head_dim // 2
    inv_freq = np.float32(ROPE_THETA) ** (np.float32(-2.0) * np.arange(half, dtype=np.float32) / np.float32(head_dim))
    freq = jnp.asarray(np.concatenate([inv_freq, inv_freq])[None], jnp.float32)
    tile, chunk, slots = 512, 16, 3
    n_chunks = tokens // chunk
    vmem = pl.BlockSpec(memory_space=pltpu.VMEM)
    hbm = pl.BlockSpec(memory_space=pl.ANY)
    return pl.pallas_call(
        functools.partial(attn_kernel, kv_heads=kv_heads, tile=tile, chunk=chunk),
        out_shape=(
            jax.ShapeDtypeStruct((tokens, n_heads * head_dim), jnp.bfloat16),
            jax.ShapeDtypeStruct(k_cache.shape, jnp.bfloat16),
            jax.ShapeDtypeStruct(v_cache.shape, jnp.bfloat16),
        ),
        in_specs=[pl.BlockSpec(memory_space=pltpu.SMEM)] + [vmem] * 4 + [hbm] * 5,
        out_specs=(vmem, hbm, hbm),
        scratch_shapes=[
            pltpu.VMEM((tokens, d_model), jnp.bfloat16),
            pltpu.VMEM((slots, d_model, tile), jnp.bfloat16),
            pltpu.VMEM(k_cache.shape, jnp.bfloat16),
            pltpu.VMEM(v_cache.shape, jnp.bfloat16),
            pltpu.VMEM((all_heads * (tokens + 8), head_dim), jnp.float32),
            pltpu.VMEM((n_heads * (tokens + 8), head_dim), jnp.float32),
            pltpu.VMEM((tokens, head_dim), jnp.float32),
            pltpu.VMEM((tokens, head_dim), jnp.float32),
            pltpu.VMEM((1, d_model), jnp.float32),
            pltpu.SemaphoreType.DMA((slots,)),
            pltpu.SemaphoreType.DMA((n_chunks,)),
            pltpu.SemaphoreType.DMA((n_chunks,)),
            pltpu.SemaphoreType.DMA((n_chunks,)),
            pltpu.SemaphoreType.DMA((n_chunks,)),
        ],
        compiler_params=pltpu.CompilerParams(vmem_limit_bytes=VMEM_LIMIT),
        name="attend",
    )(seq_lens, hidden, attn_gain.reshape(-1, 128), seq_lens.reshape(1, tokens), freq, w_query, w_key, w_value, k_cache, v_cache)


MESH_ID = pl.DeviceIdType.MESH


def moe_kernel(
    mix, hidden, ids_row, gain, router, wo, wg, wu, wd,
    out,
    gbuf, wdbuf, xall, rows_buf, inner, ret, sel_out, sel_in, comb, gates, gains,
    wo_sem, wg_sem, wd_sem, xsend, xrecv, sel_send, sel_recv, ysend, yrecv,
    *, n_ep, tile, cap,
):
    tokens, d_model = hidden.shape
    d_ff = wg.shape[1]
    local = wg.shape[0]
    n_experts = local * n_ep
    tiles = d_model // tile
    ring = n_ep // 2
    slab = local * cap
    near = 6 * cap
    f32, bf16 = jnp.float32, jnp.bfloat16
    last = (((1,), (1,)), ((), ()))

    me = lax.axis_index('ep')
    x, c = me // 2, lax.rem(me, 2)

    def at(step, core):
        return lax.rem(x + step, ring) * 2 + core

    other = 1 - c
    peers = [me, at(0, other), at(ring - 1, c), at(ring - 1, other), at(1, c), at(1, other), at(2, c), at(2, other)]
    partner, left, left2, right, right2, far, far2 = peers[1:]

    def cols(i):
        return pl.ds(pl.multiple_of(i * tile, tile), tile)

    parts = d_model // tile

    def wo_start(i, slot):
        for j in range(parts):
            span = slice(j * tile, (j + 1) * tile)
            pltpu.make_async_copy(wo.at[span, cols(i)], gbuf.at[slot, 0:tile, span], wo_sem.at[slot]).start()

    def wo_wait(slot):
        pltpu.make_async_copy(wo.at[0:tile, :], gbuf.at[slot, 0:tile, :], wo_sem.at[slot]).wait()

    def ff_copy(g):
        src = wg if g % 2 == 0 else wu
        return pltpu.make_async_copy(src.at[g // 2], gbuf.at[g], wg_sem.at[g])

    wd_slots = wdbuf.shape[0]
    wd_total = 2 * local * tiles

    def wd_copy(q):
        e = lax.rem(q // tiles, local)
        slot = lax.rem(q, wd_slots)
        return pltpu.make_async_copy(wd.at[e, :, cols(lax.rem(q, tiles))], wdbuf.at[slot], wd_sem.at[slot])

    for i in range(4):
        wo_start(i, i)

    barrier = pltpu.get_barrier_semaphore()
    for peer in peers[1:]:
        pl.semaphore_signal(barrier, inc=1, device_id={'ep': peer}, device_id_type=MESH_ID)
    pl.semaphore_wait(barrier, n_ep - 1)

    t_sub = lax.broadcasted_iota(jnp.int32, (tokens, tokens), 0)
    t_lane = lax.broadcasted_iota(jnp.int32, (tokens, tokens), 1)
    id0_row, id1_row = ids_row[0:1, :].astype(f32), ids_row[1:2, :].astype(f32)
    e_sub = lax.broadcasted_iota(jnp.int32, (n_experts, tokens), 0).astype(f32)
    spread_gain(gain, gains)
    hit_row = jnp.logical_or(e_sub == id0_row, e_sub == id1_row).astype(f32).astype(bf16)
    rank_row = jnp.dot(hit_row, (t_sub < t_lane).astype(f32).astype(bf16), preferred_element_type=f32)
    slots_row = []
    for ident in (id0_row, id1_row):
        rank = jnp.sum(jnp.where(e_sub == ident, rank_row, 0.0), axis=0, keepdims=True)
        slots_row.append(ident * cap + rank)
    for d in range(n_ep):
        want = (lax.broadcasted_iota(jnp.int32, (slab, tokens), 0) + d * slab).astype(f32)
        pick = jnp.logical_or(want == slots_row[0], want == slots_row[1])
        sel_out[d] = pick.astype(f32).astype(bf16)
    for k in range(1, n_ep):
        pltpu.make_async_remote_copy(
            src_ref=sel_out.at[peers[k]], dst_ref=sel_in.at[me], send_sem=sel_send, recv_sem=sel_recv,
            device_id={'ep': peers[k]}, device_id_type=MESH_ID,
        ).start()
    sel_in[me] = sel_out[me]

    id0, id1 = column_of(id0_row)[:, 0:1], column_of(id1_row)[:, 0:1]
    e_lane = lax.broadcasted_iota(jnp.int32, (tokens, n_experts), 1).astype(f32)
    hit = jnp.logical_or(e_lane == id0, e_lane == id1).astype(f32).astype(bf16)
    rank_col = jnp.dot((t_lane < t_sub).astype(f32).astype(bf16), hit, preferred_element_type=f32)
    s_lane = lax.broadcasted_iota(jnp.int32, (tokens, n_experts * cap), 1).astype(f32)
    for k, ident in enumerate((id0, id1)):
        rank = jnp.sum(jnp.where(e_lane == ident, rank_col, 0.0), axis=1, keepdims=True)
        comb[k * tokens:(k + 1) * tokens, :] = (s_lane == ident * cap + rank).astype(f32).astype(bf16)

    def x_copy(src, i, dev, kind):
        return pltpu.make_async_remote_copy(
            src_ref=xall.at[src, i], dst_ref=xall.at[src, i], send_sem=xsend.at[kind, i], recv_sem=xrecv.at[src, i],
            device_id={'ep': dev}, device_id_type=MESH_ID,
        )

    def arrived(src, i):
        pltpu.make_async_copy(xall.at[src, i], xall.at[src, i], xrecv.at[src, i]).wait()

    def project(i, carry):
        slot = lax.rem(i, 4)
        wo_wait(slot)
        acc = jnp.zeros((tokens, tile), f32)
        for j in range(parts):
            span = slice(j * tile, (j + 1) * tile)
            acc = acc + jnp.dot(mix[:, span], gbuf[slot, 0:tile, span], preferred_element_type=f32)
        xall[me, i] = (hidden[:, cols(i)].astype(f32) + acc).astype(bf16)
        x_copy(me, i, right, 0).start()
        x_copy(me, i, left, 1).start()
        x_copy(me, i, partner, 2).start()

        @pl.when(i < 4)
        def _():
            wo_start(i + 4, slot)

        for g in range(4):
            @pl.when(i == g + 4)
            def _():
                ff_copy(g).start()
        return carry

    lax.fori_loop(0, tiles, project, 0)
    for q in range(wd_slots):
        wd_copy(jnp.int32(q)).start()

    def square(i, acc):
        v = xall[me, i].astype(f32)
        return acc + jnp.sum(v * v, axis=1, keepdims=True)

    inv = lax.rsqrt(lax.fori_loop(0, tiles, square, jnp.zeros((tokens, 1), f32)) / d_model + NORM_EPS)

    def route(i, acc):
        v = (xall[me, i].astype(f32) * inv * gains[:, cols(i)]).astype(bf16)
        return acc + lax.dot_general(v, router[:, cols(i)], last, preferred_element_type=f32)

    logits = lax.fori_loop(0, tiles, route, jnp.zeros((tokens, n_experts), f32))
    l0 = jnp.sum(jnp.where(e_lane == id0, logits, 0.0), axis=1, keepdims=True)
    l1 = jnp.sum(jnp.where(e_lane == id1, logits, 0.0), axis=1, keepdims=True)
    top = jnp.maximum(l0, l1)
    e0, e1 = jnp.exp(l0 - top), jnp.exp(l1 - top)
    gates[0] = jnp.broadcast_to(e0 / (e0 + e1), (tokens, 128))
    gates[1] = jnp.broadcast_to(e1 / (e0 + e1), (tokens, 128))

    def gather(src, pos, i):
        got = jnp.dot(sel_in[src], xall[src, i], preferred_element_type=f32).astype(bf16)
        for e in range(local):
            rows_buf[e, pos * cap:(pos + 1) * cap, cols(i)] = got[e * cap:(e + 1) * cap]

    pltpu.make_async_copy(sel_in.at[pl.ds(0, n_ep - 1)], sel_in.at[pl.ds(0, n_ep - 1)], sel_recv).wait()

    def own(i, carry):
        gather(me, 0, i)
        return carry

    lax.fori_loop(0, tiles, own, 0)

    def neighbours(i, carry):
        arrived(left, i)
        x_copy(left, i, partner, 4).start()

        @pl.when(lax.rem(i, 2) == 0)
        def _():
            x_copy(left, i, right, 3).start()

        gather(left, 2, i)
        arrived(right, i)
        x_copy(right, i, partner, 5).start()

        @pl.when(lax.rem(i, 2) == 1)
        def _():
            x_copy(right, i, left, 3).start()

        gather(right, 4, i)
        arrived(partner, i)
        gather(partner, 1, i)
        return carry

    lax.fori_loop(0, tiles, neighbours, 0)

    def neighbours2(i, carry):
        arrived(left2, i)
        gather(left2, 3, i)
        arrived(right2, i)
        gather(right2, 5, i)
        return carry

    lax.fori_loop(0, tiles, neighbours2, 0)

    def across(i, carry):
        arrived(far, i)
        x_copy(far, i, partner, 6).start()
        gather(far, 6, i)
        return carry

    def across2(i, carry):
        arrived(far2, i)
        gather(far2, 7, i)
        return carry

    block = 16

    def normalise(first, count):
        def step(r, carry):
            rows = pl.ds(pl.multiple_of(first + r * block, block), block)
            for e in range(local):
                acc = jnp.zeros((block, tile), f32)
                for i in range(tiles):
                    v = rows_buf[e, rows, i * tile:(i + 1) * tile].astype(f32)
                    acc = acc + v * v
                scale = lax.rsqrt(jnp.sum(acc, axis=1, keepdims=True) / d_model + NORM_EPS)
                for i in range(tiles):
                    span = slice(i * tile, (i + 1) * tile)
                    v = rows_buf[e, rows, span].astype(f32)
                    rows_buf[e, rows, span] = (v * scale * gains[:, span]).astype(bf16)
            return carry

        lax.fori_loop(0, count // block, step, 0)

    def expand(e, first, count, fetched):
        for g in (2 * e, 2 * e + 1):
            if not fetched:
                ff_copy(g).wait()
        for lo in range(0, d_ff, 512):
            hi = min(lo + 512, d_ff)
            up_in = rows_buf[e, first:first + count, :]
            gate = lax.dot_general(up_in, gbuf[2 * e, lo:hi, :], last, preferred_element_type=f32)
            up = lax.dot_general(up_in, gbuf[2 * e + 1, lo:hi, :], last, preferred_element_type=f32)
            inner[first:first + count, lo:hi] = (jax.nn.silu(gate) * up).astype(bf16)

    def y_copy(e, i, pos):
        return pltpu.make_async_remote_copy(
            src_ref=rows_buf.at[e, pl.ds(pos * cap, cap), cols(i)],
            dst_ref=ret.at[pl.ds(pl.multiple_of((me * local + e) * cap, cap), cap), cols(i)],
            send_sem=ysend.at[e, i], recv_sem=yrecv.at[e, i],
            device_id={'ep': peers[pos]}, device_id_type=MESH_ID,
        )

    def contract(e, first, count, base):
        def step(i, carry):
            q = base + i
            wd_copy(q).wait()
            y = jnp.dot(inner[first:first + count, :], wdbuf[lax.rem(q, wd_slots)], preferred_element_type=f32).astype(bf16)

            @pl.when(q + wd_slots < wd_total)
            def _():
                wd_copy(q + wd_slots).start()

            rows_buf[e, first:first + count, cols(i)] = y
            if first == 0:
                ret[pl.ds(pl.multiple_of((me * local + e) * cap, cap), cap), cols(i)] = y[:cap]
            for pos in range(max(first // cap, 1), (first + count) // cap):
                y_copy(e, i, pos).start()
            return carry

        lax.fori_loop(0, tiles, step, 0)

    rest = n_ep * cap - near
    normalise(0, near)
    expand(0, 0, near, False)
    lax.fori_loop(0, tiles // 2, across, 0)
    contract(0, 0, near, 0)
    expand(1, 0, near, False)
    lax.fori_loop(tiles // 2, tiles, across, 0)
    contract(1, 0, near, tiles)
    lax.fori_loop(0, tiles, across2, 0)
    normalise(near, rest)
    expand(0, near, rest, True)
    contract(0, near, rest, 2 * tiles)
    expand(1, near, rest, True)
    contract(1, near, rest, 3 * tiles)

    whole = pl.ds(0, (n_ep - 1) * cap)

    def finish(i, carry):
        for e in range(local):
            pltpu.make_async_copy(ret.at[whole, cols(i)], ret.at[whole, cols(i)], yrecv.at[e, i]).wait()
        picked = jnp.dot(comb[...], ret[:, cols(i)], preferred_element_type=f32)
        reps = tile // 128
        g0 = jnp.concatenate([gates[0]] * reps, axis=1)
        g1 = jnp.concatenate([gates[1]] * reps, axis=1)
        out[:, cols(i)] = (xall[me, i].astype(f32) + (g0 * picked[:tokens] + g1 * picked[tokens:])).astype(bf16)
        return carry

    lax.fori_loop(0, tiles, finish, 0)

    def drain(i, carry):
        for kind in (0, 1, 2, 3, 4, 5, 6):
            pltpu.make_async_copy(xall.at[0, i], xall.at[0, i], xsend.at[kind, i]).wait()
        for e in range(local):
            pltpu.make_async_copy(ret.at[whole, cols(i)], ret.at[whole, cols(i)], ysend.at[e, i]).wait()
        return carry

    lax.fori_loop(0, tiles, drain, 0)
    pltpu.make_async_copy(sel_in.at[pl.ds(0, n_ep - 1)], sel_in.at[pl.ds(0, n_ep - 1)], sel_send).wait()


def moe(mix, hidden, expert_ids, ffn_gain, w_out, w_router, w_gate, w_up, w_down, n_ep):
    tokens, d_model = hidden.shape
    local, _, d_ff = w_gate.shape
    n_experts = local * n_ep
    cap = 4 * tokens // n_experts
    tile = 512
    tiles = d_model // tile
    vmem = pl.BlockSpec(memory_space=pltpu.VMEM)
    hbm = pl.BlockSpec(memory_space=pl.ANY)
    dma = pltpu.SemaphoreType.DMA
    return pl.pallas_call(
        functools.partial(moe_kernel, n_ep=n_ep, tile=tile, cap=cap),
        out_shape=jax.ShapeDtypeStruct((tokens, d_model), jnp.bfloat16),
        in_specs=[vmem] * 5 + [hbm] * 4,
        out_specs=vmem,
        scratch_shapes=[
            pltpu.VMEM((2 * local, d_ff, d_model), jnp.bfloat16),
            pltpu.VMEM((4, d_ff, tile), jnp.bfloat16),
            pltpu.VMEM((n_ep, tiles, tokens, tile), jnp.bfloat16),
            pltpu.VMEM((local, n_ep * cap, d_model), jnp.bfloat16),
            pltpu.VMEM((n_ep * cap, d_ff), jnp.bfloat16),
            pltpu.VMEM((n_experts * cap, d_model), jnp.bfloat16),
            pltpu.VMEM((n_ep, local * cap, tokens), jnp.bfloat16),
            pltpu.VMEM((n_ep, local * cap, tokens), jnp.bfloat16),
            pltpu.VMEM((2 * tokens, n_experts * cap), jnp.bfloat16),
            pltpu.VMEM((2, tokens, 128), jnp.float32),
            pltpu.VMEM((1, d_model), jnp.float32),
            dma((4,)), dma((4,)), dma((4,)),
            dma((7, tiles)), dma((n_ep, tiles)),
            dma, dma,
            dma((local, tiles)), dma((local, tiles)),
        ],
        compiler_params=pltpu.CompilerParams(collective_id=0, has_side_effects=True, vmem_limit_bytes=VMEM_LIMIT),
        name="moe",
    )(mix, hidden, expert_ids.T, ffn_gain.reshape(-1, 128), w_router.T, w_out, w_gate.transpose(0, 2, 1), w_up.transpose(0, 2, 1), w_down)


def solution(mesh):
    n_ep = mesh.shape['ep']
    row_spec = P(('dp', 'ep'), None)
    cache_spec = P(('dp', 'ep'), None, None, None)
    expert_spec = P('ep', None, None)
    in_specs = (row_spec, cache_spec, cache_spec, P(('dp', 'ep')), row_spec, P(), P(), P(), P(), P(), P(), P(), expert_spec, expert_spec, expert_spec)
    out_specs = (row_spec, cache_spec, cache_spec)

    def device_step(hidden, k_cache, v_cache, seq_lens, expert_ids, attn_gain, w_query, w_key, w_value, w_out, ffn_gain, w_router, w_gate, w_up, w_down):
        mix, k_cache_new, v_cache_new = attention(hidden, k_cache, v_cache, seq_lens, attn_gain, w_query, w_key, w_value)
        out = moe(mix, hidden, expert_ids, ffn_gain, w_out, w_router, w_gate, w_up, w_down, n_ep)
        return out, k_cache_new, v_cache_new

    return jax.shard_map(device_step, mesh=mesh, in_specs=in_specs, out_specs=out_specs, check_vma=False)
```

time: 233 us -> 126 us (0.54)
  Pallas kernels: 0 us -> 123 us
  matrix products: 97.1 us -> 0 us
  blocking collectives: 54.4 us -> 0 us
  waiting for transfers between devices: 47.9 us -> 0 us
  other arithmetic: 20.7 us -> 0 us
  starting transfers between devices: 5.55 us -> 0 us
  local copies, waits for them, and re-layouts: 6.02 us -> 2.29 us
    pallas_call x0 -> x2, Pallas kernels: none -> 123 us  [the longest x1 93.7 us: moe(): pl.pallas_call(functools.partial(moe_kernel, n_ep=n_ep, tile=tile, cap=ca...]
    dot_general x11 -> x0, matrix products: 87.7 us -> none  [the longest x1 16.6 us: device_step(): jnp.einsum('sxcd,xdf->sxcf', recv_buf, w_up, preferred_element_type=jnp.f...]
    all_to_all x1 -> x0, blocking collectives: 54.4 us -> none  [device_step(): recv_buf = lax.all_to_all(send_buf, 'ep', 0, 0, tiled=True)]
    all_to_all x1 -> x0, waiting for transfers between devices: 47.9 us -> none  [device_step(): lax.all_to_all(expert_out, 'ep', 0, 0, tiled=True)]
    select_n x1 -> x0, other arithmetic: 11.9 us -> none  [attention_block(): k_cache_new = jnp.where(slot_hit, key_new[:, None], k_cache)]
    sub x1 -> x0, matrix products: 9.38 us -> none  [attention_block(): jax.nn.softmax(jnp.where(visible, scores, -jnp.inf), axis=-1)]
    all_to_all x1 -> x0, starting transfers between devices: 5.55 us -> none  [device_step(): lax.all_to_all(expert_out, 'ep', 0, 0, tiled=True)]
    convert_element_type x5 -> x0, other arithmetic: 3.35 us -> none  [the longest x2 1.4 us: rms_scale(): gain_vec.astype(jnp.float32)]
  transfers between devices with their start and end apart: 1 -> 0, of which waited for: 1 -> 0; matrix products, arithmetic and copies ran while one was open for 0% -> 0% of each run, Pallas kernels for 0% -> 0%
where the time goes in v1:
time: 126 us
  Pallas kernels  123 us (98%)
  local copies, waits for them, and re-layouts  2.29 us (2%)
    pallas_call x1, Pallas kernels, moe(): pl.pallas_call(functools.partial(moe_kernel, n_ep=n_ep, tile=tile, cap=ca...  93.7 us
    pallas_call x1, Pallas kernels, attention(): pl.pallas_call(functools.partial(attn_kernel, kv_heads=kv_heads, tile=til...  29 us

profile of v1, /device:TPU:81, one launch (start us, length us, event | category | flops | bytes accessed | tf_op | source)
XLA Modules:
  0.0 125.6 jit_solution(13432801465266394569)
XLA Ops:
  0.6 29.0 %attend.1 = (bf16[128,4096]{1,0:T(8,128)(2,1)}, bf16[128,32,8,128]{3,2,1,0:T(8,128)(2,1)}, bf16[128,32,8,128]{3,2,1,0:T(8,128)(2,1)}) custom-call(s32[128]{0:T(128)} %lens.1, bf16[128,4096]{1,0:T(8,128)(2,1)} %hidden.3, bf16[32,128]{1,0:T(8,128)(2,1)} %bitcast.10, s32[1,128]{1,0:T(1,128)} %bitcast.12, f32[1,128]{1,0:T(1,128)} %constant.2.clone.freq, ...), custom_call_target="tpu_custom_call" | custom-call | tf_op jit(solution)/shard_map/attend/pallas_call | solution.py:158
  29.6 93.7 %moe.1 = bf16[128,4096]{1,0:T(8,128)(2,1)} custom-call(bf16[128,4096]{1,0:T(8,128)(2,1)} %get-tuple-element.6.mix, bf16[128,4096]{1,0:T(8,128)(2,1)} %hidden.3, s32[2,128]{1,0:T(2,128)} %bitcast.13, bf16[32,128]{1,0:T(8,128)(2,1)} %bitcast.11, bf16[16,4096]{1,0:T(8,128)(2,1)} %bitcast.9, bf16[4096,4096]{1,0:T(8,128)(2,1)} %wo.1, ...), custom_call_target="tpu_custom_call" | custom-call | tf_op jit(solution)/shard_map/moe/pallas_call | solution.py:499
  123.3 2.3 %copy.20 = bf16[128,4096]{1,0:T(8,128)(2,1)} copy(bf16[128,4096]{1,0:T(8,128)(2,1)} %moe.1) | data formatting | bytes 2097152

commit v2 on v1

--- a/solution.py
+++ b/solution.py
@@ -202,7 +202,6 @@
     tiles = d_model // tile
     ring = n_ep // 2
     slab = local * cap
-    near = 6 * cap
     f32, bf16 = jnp.float32, jnp.bfloat16
     last = (((1,), (1,)), ((), ()))
 
@@ -234,7 +233,7 @@
         return pltpu.make_async_copy(src.at[g // 2], gbuf.at[g], wg_sem.at[g])
 
     wd_slots = wdbuf.shape[0]
-    wd_total = 2 * local * tiles
+    wd_total = local * tiles
 
     def wd_copy(q):
         e = lax.rem(q // tiles, local)
@@ -408,16 +407,20 @@
 
         lax.fori_loop(0, count // block, step, 0)
 
-    def expand(e, first, count, fetched):
-        for g in (2 * e, 2 * e + 1):
-            if not fetched:
-                ff_copy(g).wait()
-        for lo in range(0, d_ff, 512):
-            hi = min(lo + 512, d_ff)
-            up_in = rows_buf[e, first:first + count, :]
-            gate = lax.dot_general(up_in, gbuf[2 * e, lo:hi, :], last, preferred_element_type=f32)
-            up = lax.dot_general(up_in, gbuf[2 * e + 1, lo:hi, :], last, preferred_element_type=f32)
-            inner[first:first + count, lo:hi] = (jax.nn.silu(gate) * up).astype(bf16)
+    def expand(e):
+        def narrow(lo, size):
+            up_in = rows_buf[e]
+            gate = lax.dot_general(up_in, gbuf[2 * e, pl.ds(lo, size), :], last, preferred_element_type=f32)
+            up = lax.dot_general(up_in, gbuf[2 * e + 1, pl.ds(lo, size), :], last, preferred_element_type=f32)
+            inner[:, pl.ds(lo, size)] = (jax.nn.silu(gate) * up).astype(bf16)
+
+        def step(n, carry):
+            narrow(pl.multiple_of(n * 128, 128), 128)
+            return carry
+
+        lax.fori_loop(0, d_ff // 128, step, 0)
+        if d_ff % 128:
+            narrow(d_ff // 128 * 128, d_ff % 128)
 
     def y_copy(e, i, pos):
         return pltpu.make_async_remote_copy(
@@ -427,39 +430,36 @@
             device_id={'ep': peers[pos]}, device_id_type=MESH_ID,
         )
 
-    def contract(e, first, count, base):
+    def contract(e):
         def step(i, carry):
-            q = base + i
+            q = e * tiles + i
             wd_copy(q).wait()
-            y = jnp.dot(inner[first:first + count, :], wdbuf[lax.rem(q, wd_slots)], preferred_element_type=f32).astype(bf16)
+            y = jnp.dot(inner[...], wdbuf[lax.rem(q, wd_slots)], preferred_element_type=f32).astype(bf16)
 
             @pl.when(q + wd_slots < wd_total)
             def _():
                 wd_copy(q + wd_slots).start()
 
-            rows_buf[e, first:first + count, cols(i)] = y
-            if first == 0:
-                ret[pl.ds(pl.multiple_of((me * local + e) * cap, cap), cap), cols(i)] = y[:cap]
-            for pos in range(max(first // cap, 1), (first + count) // cap):
+            rows_buf[e, :, cols(i)] = y
+            ret[pl.ds(pl.multiple_of((me * local + e) * cap, cap), cap), cols(i)] = y[:cap]
+            for pos in range(1, n_ep):
                 y_copy(e, i, pos).start()
             return carry
 
         lax.fori_loop(0, tiles, step, 0)
 
-    rest = n_ep * cap - near
-    normalise(0, near)
-    expand(0, 0, near, False)
-    lax.fori_loop(0, tiles // 2, across, 0)
-    contract(0, 0, near, 0)
-    expand(1, 0, near, False)
-    lax.fori_loop(tiles // 2, tiles, across, 0)
-    contract(1, 0, near, tiles)
+    lax.fori_loop(0, tiles, across, 0)
     lax.fori_loop(0, tiles, across2, 0)
-    normalise(near, rest)
-    expand(0, near, rest, True)
-    contract(0, near, rest, 2 * tiles)
-    expand(1, near, rest, True)
-    contract(1, near, rest, 3 * tiles)
+    normalise(0, n_ep * cap)
+    for g in range(2 * local):
+        ff_copy(g).wait()
+
+    def serve(e, carry):
+        expand(e)
+        contract(e)
+        return carry
+
+    lax.fori_loop(0, local, serve, 0)
 
     whole = pl.ds(0, (n_ep - 1) * cap)
 
@@ -470,7 +470,7 @@
         reps = tile // 128
         g0 = jnp.concatenate([gates[0]] * reps, axis=1)
         g1 = jnp.concatenate([gates[1]] * reps, axis=1)
-        out[:, cols(i)] = (xall[me, i].astype(f32) + (g0 * picked[:tokens] + g1 * picked[tokens:])).astype(bf16)
+        out[:, cols(i)] = xall[me, i].astype(f32) + (g0 * picked[:tokens] + g1 * picked[tokens:])
         return carry
 
     lax.fori_loop(0, tiles, finish, 0)
@@ -498,7 +498,7 @@
     dma = pltpu.SemaphoreType.DMA
     return pl.pallas_call(
         functools.partial(moe_kernel, n_ep=n_ep, tile=tile, cap=cap),
-        out_shape=jax.ShapeDtypeStruct((tokens, d_model), jnp.bfloat16),
+        out_shape=jax.ShapeDtypeStruct((tokens, d_model), jnp.float32),
         in_specs=[vmem] * 5 + [hbm] * 4,
         out_specs=vmem,
         scratch_shapes=[
@@ -523,6 +523,473 @@
     )(mix, hidden, expert_ids.T, ffn_gain.reshape(-1, 128), w_router.T, w_out, w_gate.transpose(0, 2, 1), w_up.transpose(0, 2, 1), w_down)
 
 
+def packed_kernel(
+    mix, hidden, ids_row, gain, router, wo, wg, wu, wd,
+    out, fits,
+    gbuf, wdbuf, xown, xmate, stage, xin, rows_buf, wide_acc, inner, ret, ycross, ystage,
+    slots_out, slots_in, spread, own_sel, sel, pack, comb, gates, gains, scale_out, scale_in, row_scale,
+    wo_sem, wg_sem, wd_sem, slot_send, slot_recv, near_send, far_send, mate_send, fwd_send, x_recv, mate_recv,
+    ysend_mate, yrecv_mate, cross_send, cross_recv, ysend, yrecv, scale_send, scale_recv,
+    *, n_ep, tile, cap, room,
+):
+    tokens, d_model = hidden.shape
+    d_ff = wg.shape[1]
+    local = wg.shape[0]
+    n_experts = local * n_ep
+    tiles = d_model // tile
+    ring = n_ep // 2
+    slab = local * cap
+    chip_slab = 2 * slab
+    f32, bf16 = jnp.float32, jnp.bfloat16
+    last = (((1,), (1,)), ((), ()))
+
+    me = lax.axis_index('ep')
+    x, c = me // 2, lax.rem(me, 2)
+    other = 1 - c
+
+    def at(step, core):
+        return lax.rem(x + step, ring) * 2 + core
+
+    mate = at(0, other)
+    places = [at(3, c), at(3, other), at(1, c), at(1, other), at(2, c), at(2, other)]
+    peers = [mate] + places
+
+    def cols(i):
+        return pl.ds(pl.multiple_of(i * tile, tile), tile)
+
+    def to(dev):
+        return {'device_id': {'ep': dev}, 'device_id_type': MESH_ID}
+
+    def landed(ref, sem):
+        pltpu.make_async_copy(ref, ref, sem).wait()
+
+    parts = d_model // tile
+
+    def wo_start(i, slot):
+        for j in range(parts):
+            span = slice(j * tile, (j + 1) * tile)
+            pltpu.make_async_copy(wo.at[span, cols(i)], gbuf.at[slot, 0:tile, span], wo_sem.at[slot]).start()
+
+    def wo_wait(slot):
+        pltpu.make_async_copy(wo.at[0:tile, :], gbuf.at[slot, 0:tile, :], wo_sem.at[slot]).wait()
+
+    def ff_copy(g):
+        src = wg if g % 2 == 0 else wu
+        return pltpu.make_async_copy(src.at[g // 2], gbuf.at[g], wg_sem.at[g])
+
+    wd_slots = wdbuf.shape[0]
+    wd_total = local * tiles
+
+    def tile_of(q):
+        k = lax.rem(q // local, tiles)
+        return 2 * (k // 2) + lax.rem(other + lax.rem(k, 2), 2)
+
+    def wd_get(q):
+        slot = lax.rem(q, wd_slots)
+        return pltpu.make_async_copy(wd.at[lax.rem(q, local), :, cols(tile_of(q))], wdbuf.at[slot], wd_sem.at[slot])
+
+    def wd_wait(q):
+        wd_get(q).wait()
+
+    def wd_next(q):
+        @pl.when(q + wd_slots < wd_total)
+        def _():
+            wd_get(q + wd_slots).start()
+
+    for i in range(4):
+        wo_start(i, i)
+
+    barrier = pltpu.get_barrier_semaphore()
+    for peer in peers:
+        pl.semaphore_signal(barrier, inc=1, device_id={'ep': peer}, device_id_type=MESH_ID)
+
+    t_sub = lax.broadcasted_iota(jnp.int32, (tokens, tokens), 0)
+    t_lane = lax.broadcasted_iota(jnp.int32, (tokens, tokens), 1)
+    before = (t_sub < t_lane).astype(f32).astype(bf16)
+    id0_row, id1_row = ids_row[0:1, :].astype(f32), ids_row[1:2, :].astype(f32)
+    e_sub = lax.broadcasted_iota(jnp.int32, (n_experts, tokens), 0).astype(f32)
+    spread_gain(gain, gains)
+    hit_row = jnp.logical_or(e_sub == id0_row, e_sub == id1_row).astype(f32).astype(bf16)
+    rank_row = jnp.dot(hit_row, before, preferred_element_type=f32)
+    slots_row = []
+    for ident in (id0_row, id1_row):
+        rank = jnp.sum(jnp.where(e_sub == ident, rank_row, 0.0), axis=0, keepdims=True)
+        slots_row.append(ident * cap + rank)
+    eight = lax.broadcasted_iota(jnp.int32, (8, tokens), 0)
+    slots_out[...] = jnp.where(eight == 0, slots_row[0], slots_row[1])
+
+    def inside(slot, chip):
+        low = (chip * chip_slab).astype(f32) if not isinstance(chip, int) else float(chip * chip_slab)
+        return jnp.logical_and(slot >= low, slot < low + chip_slab).astype(f32)
+
+    def ranks(s0, s1, chip):
+        in0, in1 = inside(s0, chip), inside(s1, chip)
+        uses = jnp.maximum(in0, in1)
+        rows = jnp.where(eight == 0, uses, jnp.where(eight == 1, in0, in1))
+        got = jnp.dot(rows.astype(bf16), before, preferred_element_type=f32)
+        base = jnp.sum(in0, axis=1, keepdims=True)
+        return in0, in1, uses, got[0:1, :], got[1:2, :], base + got[2:3, :]
+
+    p_sub = lax.broadcasted_iota(jnp.int32, (room, tokens), 0).astype(f32)
+    steps = (3, 1, 2)
+    index = [jnp.zeros((1, tokens), f32), jnp.zeros((1, tokens), f32)]
+    for k, step in enumerate(steps):
+        in0, in1, uses, dpos, q0, q1 = ranks(slots_row[0], slots_row[1], lax.rem(x + step, ring))
+        spread[k] = jnp.logical_and(p_sub == dpos, uses > 0.5).astype(f32).astype(bf16)
+        index[0] = index[0] + in0 * (k * room + q0)
+        index[1] = index[1] + in1 * (k * room + q1)
+    mine_low = (x * chip_slab).astype(f32)
+    for k in range(2):
+        index[k] = index[k] + inside(slots_row[k], x) * (3 * room + slots_row[k] - mine_low)
+    width = 3 * room + chip_slab
+    w_lane = lax.broadcasted_iota(jnp.int32, (tokens, width), 1).astype(f32)
+    for k in range(2):
+        comb[k * tokens:(k + 1) * tokens, :] = (w_lane == column_of(index[k])[:, 0:1]).astype(f32).astype(bf16)
+
+    def slot_sel(dev, s0, s1):
+        want = (lax.broadcasted_iota(jnp.int32, (slab, tokens), 0) + dev * slab).astype(f32)
+        return jnp.logical_or(want == s0, want == s1).astype(f32).astype(bf16)
+
+    pl.semaphore_wait(barrier, n_ep - 1)
+    for k, peer in enumerate(peers):
+        there = (0, 3, 4, 1, 2, 5, 6)[k]
+        pltpu.make_async_remote_copy(
+            src_ref=slots_out, dst_ref=slots_in.at[there], send_sem=slot_send.at[k], recv_sem=slot_recv.at[there], **to(peer),
+        ).start()
+
+    def x_copy(place, i):
+        k, dev, there = {0: (0, places[0], 2), 2: (1, places[2], 0), 4: (2, places[4], 4)}[place]
+        sem = near_send.at[k, i] if k < 2 else far_send.at[i]
+        return pltpu.make_async_remote_copy(
+            src_ref=stage.at[k, i], dst_ref=xin.at[there, i], send_sem=sem, recv_sem=x_recv.at[there, i], **to(dev),
+        )
+
+    def mate_copy(i):
+        return pltpu.make_async_remote_copy(
+            src_ref=xown.at[i], dst_ref=xmate.at[i], send_sem=mate_send.at[i], recv_sem=mate_recv.at[i], **to(mate),
+        )
+
+    def fwd_copy(place, i):
+        return pltpu.make_async_remote_copy(
+            src_ref=xin.at[place, i], dst_ref=xin.at[place + 1, i], send_sem=fwd_send.at[place // 2, i],
+            recv_sem=x_recv.at[place + 1, i], **to(mate),
+        )
+
+    own_sel[0] = slot_sel(me, slots_row[0], slots_row[1])
+    c_lane = lax.broadcasted_iota(jnp.int32, (chip_slab, tokens), 0)
+    want = (lax.rem(c_lane + c * slab, chip_slab) + x * chip_slab).astype(f32)
+
+    def learn(k):
+        landed(slots_in.at[k], slot_recv.at[k])
+        s0, s1 = slots_in[k, 0:1, :], slots_in[k, 1:2, :]
+        own_sel[k + 1] = slot_sel(me, s0, s1)
+        in0, in1, uses, dpos, q0, q1 = ranks(s0, s1, x)
+        put = jnp.logical_and(p_sub == dpos, uses > 0.5).astype(f32).astype(bf16)
+        sel[k] = lax.dot_general(own_sel[k + 1], put, last, preferred_element_type=f32).astype(bf16)
+        total = jnp.zeros((room, chip_slab), f32)
+        for s, inn, q in ((s0, in0, q0), (s1, in1, q1)):
+            spot = jnp.logical_and(p_sub == q, inn > 0.5).astype(f32).astype(bf16)
+            total = total + lax.dot_general(spot, (want == s).astype(f32).astype(bf16), last, preferred_element_type=f32)
+        pack[k] = total.astype(bf16)
+
+    def project(i, carry):
+        slot = lax.rem(i, 4)
+        wo_wait(slot)
+        acc = jnp.zeros((tokens, tile), f32)
+        for j in range(parts):
+            span = slice(j * tile, (j + 1) * tile)
+            acc = acc + jnp.dot(mix[:, span], gbuf[slot, 0:tile, span], preferred_element_type=f32)
+        xt = (hidden[:, cols(i)].astype(f32) + acc).astype(bf16)
+        xown[i] = xt
+        for k in range(3):
+            stage[k, i] = jnp.dot(spread[k], xt, preferred_element_type=f32).astype(bf16)
+        x_copy(0, i).start()
+        x_copy(2, i).start()
+        mate_copy(i).start()
+
+        @pl.when(i < n_ep - 1)
+        def _():
+            learn(i)
+
+        wide = xt.astype(f32)
+        wide = wide * wide
+        for j in range(0, tile, 128):
+            carry = carry + wide[:, j:j + 128]
+
+        @pl.when(i < 4)
+        def _():
+            wo_start(i + 4, slot)
+
+        for g in range(4):
+            @pl.when(i == g + 4)
+            def _():
+                ff_copy(g).start()
+        return carry
+
+    sums = lax.fori_loop(0, tiles, project, jnp.zeros((tokens, 128), f32))
+    inv = lax.rsqrt(jnp.sum(sums, axis=1, keepdims=True) / d_model + NORM_EPS)
+    inv_row = jnp.broadcast_to(inv, (tokens, 128)).T[0:8, :]
+    scale_out[...] = inv_row
+    for k, peer in enumerate(peers):
+        there = (0, 3, 4, 1, 2, 5, 6)[k]
+        pltpu.make_async_remote_copy(
+            src_ref=scale_out, dst_ref=scale_in.at[there], send_sem=scale_send.at[k], recv_sem=scale_recv.at[there], **to(peer),
+        ).start()
+
+    def send_far(i, carry):
+        x_copy(4, i).start()
+        return carry
+
+    lax.fori_loop(0, tiles, send_far, 0)
+    for q in range(wd_slots):
+        wd_get(jnp.int32(q)).start()
+
+    def learn_scale(k, row):
+        hit = own_sel[k].astype(f32) * row
+        row_scale[k] = jnp.broadcast_to(jnp.sum(hit, axis=1, keepdims=True), (slab, 128))
+
+    def gather(pick, block, pos, i):
+        got = jnp.dot(pick, block, preferred_element_type=f32)
+        mul = jnp.concatenate([row_scale[pos]] * (tile // 128), axis=1)
+        got = (got * mul * gains[:, cols(i)]).astype(bf16)
+        for e in range(local):
+            rows_buf[e, pos * cap:(pos + 1) * cap, cols(i)] = got[e * cap:(e + 1) * cap]
+
+    def scale_from(k):
+        landed(scale_in.at[k], scale_recv.at[k])
+        learn_scale(k + 1, scale_in[k, 0:1, :])
+
+    learn_scale(0, inv_row[0:1, :])
+    scale_from(0)
+
+    def own(i, carry):
+        landed(xmate.at[i], mate_recv.at[i])
+        gather(own_sel[0], xown[i], 0, i)
+        gather(own_sel[1], xmate[i], 1, i)
+        for place in (0, 2):
+            landed(xin.at[place, i], x_recv.at[place, i])
+            fwd_copy(place, i).start()
+        return carry
+
+    lax.fori_loop(0, tiles, own, 0)
+    for k in range(1, 5):
+        scale_from(k)
+
+    def neighbours(i, carry):
+        for place in (1, 3):
+            landed(xin.at[place, i], x_recv.at[place, i])
+        for place in range(4):
+            gather(sel[place + 1], xin[place, i], place + 2, i)
+        return carry
+
+    lax.fori_loop(0, tiles, neighbours, 0)
+    for k in range(5, 7):
+        scale_from(k)
+
+    for g in range(2 * local):
+        ff_copy(g).wait()
+
+    def expand(i):
+        for e in range(local):
+            for k in range(2):
+                part = lax.dot_general(rows_buf[e, :, cols(i)], gbuf[2 * e + k, :, cols(i)], last, preferred_element_type=f32)
+                wide_acc[2 * e + k] = jnp.where(i == 0, part, wide_acc[2 * e + k] + part)
+
+    def last_source(i):
+        landed(xin.at[5, i], x_recv.at[5, i])
+        gather(sel[6], xin[5, i], 7, i)
+        expand(i)
+
+    def across(i, carry):
+        landed(xin.at[4, i], x_recv.at[4, i])
+        fwd_copy(4, i).start()
+        gather(sel[5], xin[4, i], 6, i)
+
+        @pl.when(i > 0)
+        def _():
+            last_source(i - 1)
+        return carry
+
+    lax.fori_loop(0, tiles, across, 0)
+    last_source(tiles - 1)
+    for e in range(local):
+        inner[e] = (jax.nn.silu(wide_acc[2 * e]) * wide_acc[2 * e + 1]).astype(bf16)
+
+
+    def mate_y(e, i):
+        return pltpu.make_async_remote_copy(
+            src_ref=rows_buf.at[e, pl.ds(cap, cap), cols(i)],
+            dst_ref=ret.at[pl.ds(pl.multiple_of(3 * room + c * slab + e * cap, cap // 2), cap), cols(i)],
+            send_sem=ysend_mate.at[e, i], recv_sem=yrecv_mate.at[e, i], **to(mate),
+        )
+
+    lead = 2 * cap
+
+    def cross_y(e, i):
+        rows = pl.ds(lead, n_ep * cap - lead)
+        return pltpu.make_async_remote_copy(
+            src_ref=rows_buf.at[e, rows, cols(i)], dst_ref=ycross.at[i // 2, e, rows],
+            send_sem=cross_send.at[e, i // 2], recv_sem=cross_recv.at[e, i // 2], **to(mate),
+        )
+
+    def y_copy(place, half, i):
+        there = (1, 1, 0, 0, 2, 2)[place]
+        return pltpu.make_async_remote_copy(
+            src_ref=ystage.at[place, half], dst_ref=ret.at[pl.ds(there * room, room), cols(i)],
+            send_sem=ysend.at[place, half], recv_sem=yrecv.at[there, i], **to(places[place]),
+        )
+
+    def contract():
+        def finish_pair(half):
+            i = 2 * half + c
+            for e in range(local):
+                landed(ycross.at[half, e, pl.ds(lead, n_ep * cap - lead)], cross_recv.at[e, half])
+            for pos in range(2, n_ep):
+                block_rows = slice(pos * cap, (pos + 1) * cap)
+                swapped = slice((pos ^ 1) * cap, ((pos ^ 1) + 1) * cap)
+                pieces = [rows_buf[e, block_rows, cols(i)] for e in range(local)] + [ycross[half, e, swapped, :] for e in range(local)]
+                ystage[pos - 2, half] = jnp.dot(pack[pos - 1], jnp.concatenate(pieces, axis=0), preferred_element_type=f32).astype(bf16)
+                y_copy(pos - 2, half, i).start()
+
+        def pair(half, carry):
+            for k in range(2):
+                i = 2 * half + (lax.rem(other + k, 2))
+                for e in range(local):
+                    q = (2 * half + k) * local + e
+                    wd_wait(q)
+                    y = jnp.dot(inner[e], wdbuf[lax.rem(q, wd_slots)], preferred_element_type=f32).astype(bf16)
+                    wd_next(q)
+                    rows_buf[e, :, cols(i)] = y
+                    if k == 0:
+                        cross_y(e, i).start()
+                    ret[pl.ds(pl.multiple_of(3 * room + c * slab + e * cap, cap // 2), cap), cols(i)] = y[:cap]
+                    mate_y(e, i).start()
+
+            @pl.when(half > 0)
+            def _():
+                finish_pair(half - 1)
+            return carry
+
+        lax.fori_loop(0, tiles // 2, pair, 0)
+        finish_pair(tiles // 2 - 1)
+
+    contract()
+
+    top = jnp.zeros((1, 1), f32)
+    for s0, s1 in [(slots_row[0], slots_row[1])] + [(slots_in[k, 0:1, :], slots_in[k, 1:2, :]) for k in range(n_ep - 1)]:
+        for d in range(ring):
+            top = jnp.maximum(top, jnp.sum(inside(s0, d) + inside(s1, d), axis=1, keepdims=True))
+    fits[0] = (top[0, 0] <= room).astype(jnp.int32)
+
+    def route(i, acc):
+        v = (xown[i].astype(f32) * inv * gains[:, cols(i)]).astype(bf16)
+        return acc + lax.dot_general(v, router[:, cols(i)], last, preferred_element_type=f32)
+
+    logits = lax.fori_loop(0, tiles, route, jnp.zeros((tokens, n_experts), f32))
+    e_lane = lax.broadcasted_iota(jnp.int32, (tokens, n_experts), 1).astype(f32)
+    id0, id1 = column_of(id0_row)[:, 0:1], column_of(id1_row)[:, 0:1]
+    l0 = jnp.sum(jnp.where(e_lane == id0, logits, 0.0), axis=1, keepdims=True)
+    l1 = jnp.sum(jnp.where(e_lane == id1, logits, 0.0), axis=1, keepdims=True)
+    top = jnp.maximum(l0, l1)
+    e0, e1 = jnp.exp(l0 - top), jnp.exp(l1 - top)
+    gates[0] = jnp.broadcast_to(e0 / (e0 + e1), (tokens, 128))
+    gates[1] = jnp.broadcast_to(e1 / (e0 + e1), (tokens, 128))
+
+    def finish(i, carry):
+        for e in range(local):
+            landed(ret.at[pl.ds(0, cap), cols(i)], yrecv_mate.at[e, i])
+        for k in range(3):
+            landed(ret.at[pl.ds(0, room), cols(i)], yrecv.at[k, i])
+        picked = jnp.dot(comb[...], ret[:, cols(i)], preferred_element_type=f32)
+        reps = tile // 128
+        g0 = jnp.concatenate([gates[0]] * reps, axis=1)
+        g1 = jnp.concatenate([gates[1]] * reps, axis=1)
+        out[:, cols(i)] = xown[i].astype(f32) + (g0 * picked[:tokens] + g1 * picked[tokens:])
+        return carry
+
+    lax.fori_loop(0, tiles, finish, 0)
+
+    def drain(i, carry):
+        for k in range(2):
+            landed(stage.at[0, 0], near_send.at[k, i])
+        landed(stage.at[0, 0], far_send.at[i])
+        landed(xown.at[0], mate_send.at[i])
+        for k in range(3):
+            landed(stage.at[0, 0], fwd_send.at[k, i])
+        for e in range(local):
+            landed(ret.at[pl.ds(0, cap), cols(0)], ysend_mate.at[e, i])
+        return carry
+
+    lax.fori_loop(0, tiles, drain, 0)
+
+    def drain2(half, carry):
+        for e in range(local):
+            landed(ycross.at[0, 0, pl.ds(lead, n_ep * cap - lead)], cross_send.at[e, half])
+        for place in range(6):
+            landed(ystage.at[0, 0], ysend.at[place, half])
+        return carry
+
+    lax.fori_loop(0, tiles // 2, drain2, 0)
+    for k in range(7):
+        landed(slots_out, slot_send.at[k])
+        landed(scale_out, scale_send.at[k])
+
+
+def moe_packed(mix, hidden, expert_ids, ffn_gain, w_out, w_router, w_gate, w_up, w_down, n_ep, room):
+    tokens, d_model = hidden.shape
+    local, _, d_ff = w_gate.shape
+    n_experts = local * n_ep
+    cap = 4 * tokens // n_experts
+    slab = local * cap
+    tile = 512
+    tiles = d_model // tile
+    vmem = pl.BlockSpec(memory_space=pltpu.VMEM)
+    hbm = pl.BlockSpec(memory_space=pl.ANY)
+    dma = pltpu.SemaphoreType.DMA
+    bf16 = jnp.bfloat16
+    return pl.pallas_call(
+        functools.partial(packed_kernel, n_ep=n_ep, tile=tile, cap=cap, room=room),
+        out_shape=(jax.ShapeDtypeStruct((tokens, d_model), jnp.float32), jax.ShapeDtypeStruct((1,), jnp.int32)),
+        in_specs=[vmem] * 5 + [hbm] * 4,
+        out_specs=(vmem, pl.BlockSpec(memory_space=pltpu.SMEM)),
+        scratch_shapes=[
+            pltpu.VMEM((2 * local, d_ff, d_model), bf16),
+            pltpu.VMEM((4, d_ff, tile), bf16),
+            pltpu.VMEM((tiles, tokens, tile), bf16),
+            pltpu.VMEM((tiles, tokens, tile), bf16),
+            pltpu.VMEM((3, tiles, room, tile), bf16),
+            pltpu.VMEM((6, tiles, room, tile), bf16),
+            pltpu.VMEM((local, n_ep * cap, d_model), bf16),
+            pltpu.VMEM((2 * local, n_ep * cap, d_ff), jnp.float32),
+            pltpu.VMEM((local, n_ep * cap, d_ff), bf16),
+            pltpu.VMEM((3 * room + 2 * slab, d_model), bf16),
+            pltpu.VMEM((tiles // 2, local, n_ep * cap, tile), bf16),
+            pltpu.VMEM((6, tiles // 2, room, tile), bf16),
+            pltpu.VMEM((8, tokens), jnp.float32),
+            pltpu.VMEM((7, 8, tokens), jnp.float32),
+            pltpu.VMEM((3, room, tokens), bf16),
+            pltpu.VMEM((n_ep, slab, tokens), bf16),
+            pltpu.VMEM((n_ep - 1, slab, room), bf16),
+            pltpu.VMEM((n_ep - 1, room, 2 * slab), bf16),
+            pltpu.VMEM((2 * tokens, 3 * room + 2 * slab), bf16),
+            pltpu.VMEM((2, tokens, 128), jnp.float32),
+            pltpu.VMEM((1, d_model), jnp.float32),
+            pltpu.VMEM((8, tokens), jnp.float32),
+            pltpu.VMEM((n_ep - 1, 8, tokens), jnp.float32),
+            pltpu.VMEM((n_ep, slab, 128), jnp.float32),
+            dma((4,)), dma((4,)), dma((4,)),
+            dma((7,)), dma((7,)),
+            dma((2, tiles)), dma((tiles,)), dma((tiles,)), dma((3, tiles)), dma((6, tiles)), dma((tiles,)),
+            dma((local, tiles)), dma((local, tiles)),
+            dma((local, tiles // 2)), dma((local, tiles // 2)),
+            dma((6, tiles // 2)), dma((3, tiles)),
+            dma((n_ep - 1,)), dma((n_ep - 1,)),
+        ],
+        compiler_params=pltpu.CompilerParams(collective_id=1, has_side_effects=True, vmem_limit_bytes=VMEM_LIMIT),
+        name="moe_packed",
+    )(mix, hidden, expert_ids.T, ffn_gain.reshape(-1, 128), w_router.T, w_out, w_gate.transpose(0, 2, 1), w_up.transpose(0, 2, 1), w_down)
+
+
 def solution(mesh):
     n_ep = mesh.shape['ep']
     row_spec = P(('dp', 'ep'), None)
@@ -533,7 +1000,10 @@
 
     def device_step(hidden, k_cache, v_cache, seq_lens, expert_ids, attn_gain, w_query, w_key, w_value, w_out, ffn_gain, w_router, w_gate, w_up, w_down):
         mix, k_cache_new, v_cache_new = attention(hidden, k_cache, v_cache, seq_lens, attn_gain, w_query, w_key, w_value)
-        out = moe(mix, hidden, expert_ids, ffn_gain, w_out, w_router, w_gate, w_up, w_down, n_ep)
+        operands = (mix, hidden, expert_ids, ffn_gain, w_out, w_router, w_gate, w_up, w_down)
+        room = 5 * hidden.shape[0] // 8
+        out, fits = moe_packed(*operands, n_ep, room)
+        out = lax.cond(fits[0] == 1, lambda ops: ops[0].astype(jnp.bfloat16), lambda ops: moe(*ops[1:], n_ep).astype(jnp.bfloat16), (out,) + operands)
         return out, k_cache_new, v_cache_new
 
     return jax.shard_map(device_step, mesh=mesh, in_specs=in_specs, out_specs=out_specs, check_vma=False)

time: 126 us -> 114 us (0.905)
  Pallas kernels: 123 us -> 109 us
  other arithmetic: 0 us -> 1.71 us
  local copies, waits for them, and re-layouts: 2.29 us -> 0.97 us
    pallas_call x1, Pallas kernels: 93.7 us -> 80.5 us  [moe_packed(): pl.pallas_call(functools.partial(packed_kernel, n_ep=n_ep, tile=tile, cap...]
    convert_element_type x0 -> x1, other arithmetic: none -> 1.71 us  [device_step(): moe(*ops[1:], n_ep).astype(jnp.bfloat16)]
    unnamed x1 -> x6, local copies, waits for them, and re-layouts: 2.29 us -> 0.97 us
where the time goes in v2:
time: 114 us
  Pallas kernels  109 us (96%)
  other arithmetic  1.71 us (2%)
  between operations  1.38 us (1%)
    pallas_call x1, Pallas kernels, moe_packed(): pl.pallas_call(functools.partial(packed_kernel, n_ep=n_ep, tile=tile, cap...  80.5 us
    pallas_call x1, Pallas kernels, attention(): pl.pallas_call(functools.partial(attn_kernel, kv_heads=kv_heads, tile=til...  29 us

profile of v2, /device:TPU:81, one launch (start us, length us, event | category | flops | bytes accessed | tf_op | source)
XLA Modules:
  0.0 113.8 jit_solution(13607941355790618256)
XLA Ops:
  0.6 0.0 copy-start.1
  0.6 0.0 copy-start.2
  0.7 29.0 %attend.1 = (bf16[128,4096]{1,0:T(8,128)(2,1)}, bf16[128,32,8,128]{3,2,1,0:T(8,128)(2,1)}, bf16[128,32,8,128]{3,2,1,0:T(8,128)(2,1)}) custom-call(s32[128]{0:T(128)} %lens.1, bf16[128,4096]{1,0:T(8,128)(2,1)} %hidden.3, bf16[32,128]{1,0:T(8,128)(2,1)} %bitcast.21, s32[1,128]{1,0:T(1,128)} %bitcast.24, f32[1,128]{1,0:T(1,128)} %constant.5.clone.freq, ...), custom_call_target="tpu_custom_call" | custom-call | tf_op jit(solution)/shard_map/attend/pallas_call | solution.py:158
  29.7 0.0 copy-done.1
  29.7 0.0 copy-done.2
  29.7 80.5 %moe_packed.1 = (f32[128,4096]{1,0:T(8,128)}, s32[1]{0:T(128)}) custom-call(bf16[128,4096]{1,0:T(8,128)(2,1)} %get-tuple-element.47.mix, bf16[128,4096]{1,0:T(8,128)(2,1)} %hidden.3, s32[2,128]{1,0:T(2,128)S(1)} %bitcast.22, bf16[32,128]{1,0:T(8,128)(2,1)S(1)} %bitcast.19, bf16[16,4096]{1,0:T(8,128)(2,1)} %bitcast.17, bf16[4096,4096]{1,0:T(8,128)(2,1)} %wo.1, ...), custom_call_target="tpu_custom_call" | custom-call | tf_op jit(solution)/shard_map/moe_packed/pallas_call | solution.py:950
  110.9 1.9 %conditional.5 = (bf16[128,4096]{1,0:T(8,128)(2,1)S(1)}) conditional(s32[]{:T(128)} %bitcast.12, (s32[128,2]{0,1:T(2,128)S(1)}, bf16[4096]{0:T(1024)(128)(2,1)S(1)}, bf16[4096,16]{0,1:T(8,128)(2,1)}, bf16[2,4096,960]{1,2,0:T(8,128)(2,1)}, bf16[2,4096,960]{1,2,0:T(8,128)(2,1)}, /*index=5*/bf16[128,4096]{1,0:T(8,128)(2,1)}, ...), branch_computations={%region_0.0_spmd, %region_1.0_spmd} | conditional | flops 524288 | bytes 3145736
  111.1 1.7 %convert_element_type.15 = bf16[128,4096]{1,0:T(8,128)(2,1)S(1)} convert(f32[128,4096]{1,0:T(8,128)} %param.1) | non-fusion elementwise | flops 524288 | bytes 3145728 | tf_op jit(solution)/shard_map/cond/branch_0_fun/convert_element_type | solution.py:1006
  112.8 0.0 copy-start
  112.8 1.0 copy-done
Async XLA Ops:
  0.6 29.0 %copy-start.1 = (bf16[4096]{0:T(1024)(128)(2,1)S(1)}, bf16[4096]{0:T(1024)(128)(2,1)}, u32[]{:S(2)}) copy-start(bf16[4096]{0:T(1024)(128)(2,1)} %param.28) | copy-start | bytes 24580
  0.6 29.0 %copy-start.2 = (s32[128,2]{0,1:T(2,128)S(1)}, s32[128,2]{0,1:T(2,128)}, u32[]{:S(2)}) copy-start(s32[128,2]{0,1:T(2,128)} %param.22) | copy-start | bytes 3076
  112.8 1.0 copy-start

commit v3 on v2

--- a/solution.py
+++ b/solution.py
@@ -110,6 +110,8 @@
             n = lens[t]
             kbuf[t, n] = heads[pl.ds(q_heads * pitch + t, kv_heads, stride=pitch), :].astype(jnp.bfloat16)
             vbuf[t, n] = heads[pl.ds((q_heads + kv_heads) * pitch + t, kv_heads, stride=pitch), :].astype(jnp.bfloat16)
+        pltpu.make_async_copy(kbuf.at[rows(c)], kn.at[rows(c)], kout.at[c]).start()
+        pltpu.make_async_copy(vbuf.at[rows(c)], vn.at[rows(c)], vout.at[c]).start()
         probs = []
         for j in range(chunk):
             t = base + j
@@ -126,8 +128,6 @@
             values = vbuf[t].reshape(seq_len * kv_heads, head_dim)
             o = jnp.dot(probs[j], values, preferred_element_type=jnp.float32)
             mixed[pl.ds(t, q_heads, stride=pitch), :] = o
-        pltpu.make_async_copy(kbuf.at[rows(c)], kn.at[rows(c)], kout.at[c]).start()
-        pltpu.make_async_copy(vbuf.at[rows(c)], vn.at[rows(c)], vout.at[c]).start()
         return carry
 
     lax.fori_loop(0, n_chunks, attend, 0)
@@ -529,7 +529,7 @@
     gbuf, wdbuf, xown, xmate, stage, xin, rows_buf, wide_acc, inner, ret, ycross, ystage,
     slots_out, slots_in, spread, own_sel, sel, pack, comb, gates, gains, scale_out, scale_in, row_scale,
     wo_sem, wg_sem, wd_sem, slot_send, slot_recv, near_send, far_send, mate_send, fwd_send, x_recv, mate_recv,
-    ysend_mate, yrecv_mate, cross_send, cross_recv, ysend, yrecv, scale_send, scale_recv,
+    ysend_mate, yrecv_mate, cross_send, cross_recv, ysend, yrecv, scale_send, scale_recv, done, out_sem,
     *, n_ep, tile, cap, room,
 ):
     tokens, d_model = hidden.shape
@@ -641,11 +641,6 @@
     mine_low = (x * chip_slab).astype(f32)
     for k in range(2):
         index[k] = index[k] + inside(slots_row[k], x) * (3 * room + slots_row[k] - mine_low)
-    width = 3 * room + chip_slab
-    w_lane = lax.broadcasted_iota(jnp.int32, (tokens, width), 1).astype(f32)
-    for k in range(2):
-        comb[k * tokens:(k + 1) * tokens, :] = (w_lane == column_of(index[k])[:, 0:1]).astype(f32).astype(bf16)
-
     def slot_sel(dev, s0, s1):
         want = (lax.broadcasted_iota(jnp.int32, (slab, tokens), 0) + dev * slab).astype(f32)
         return jnp.logical_or(want == s0, want == s1).astype(f32).astype(bf16)
@@ -692,6 +687,8 @@
             total = total + lax.dot_general(spot, (want == s).astype(f32).astype(bf16), last, preferred_element_type=f32)
         pack[k] = total.astype(bf16)
 
+    early = 5
+
     def project(i, carry):
         slot = lax.rem(i, 4)
         wo_wait(slot)
@@ -703,13 +700,12 @@
         xown[i] = xt
         for k in range(3):
             stage[k, i] = jnp.dot(spread[k], xt, preferred_element_type=f32).astype(bf16)
-        x_copy(0, i).start()
-        x_copy(2, i).start()
+        @pl.when(i < early)
+        def _():
+            x_copy(0, i).start()
+            x_copy(2, i).start()
+
         mate_copy(i).start()
-
-        @pl.when(i < n_ep - 1)
-        def _():
-            learn(i)
 
         wide = xt.astype(f32)
         wide = wide * wide
@@ -736,11 +732,20 @@
             src_ref=scale_out, dst_ref=scale_in.at[there], send_sem=scale_send.at[k], recv_sem=scale_recv.at[there], **to(peer),
         ).start()
 
+    def send_near(i, carry):
+        x_copy(0, i).start()
+        x_copy(2, i).start()
+        return carry
+
+    lax.fori_loop(early, tiles, send_near, 0)
+
     def send_far(i, carry):
         x_copy(4, i).start()
         return carry
 
     lax.fori_loop(0, tiles, send_far, 0)
+    for k in range(n_ep - 1):
+        learn(k)
     for q in range(wd_slots):
         wd_get(jnp.int32(q)).start()
 
@@ -760,29 +765,30 @@
         learn_scale(k + 1, scale_in[k, 0:1, :])
 
     learn_scale(0, inv_row[0:1, :])
-    scale_from(0)
-
-    def own(i, carry):
-        landed(xmate.at[i], mate_recv.at[i])
-        gather(own_sel[0], xown[i], 0, i)
-        gather(own_sel[1], xmate[i], 1, i)
-        for place in (0, 2):
-            landed(xin.at[place, i], x_recv.at[place, i])
-            fwd_copy(place, i).start()
-        return carry
-
-    lax.fori_loop(0, tiles, own, 0)
-    for k in range(1, 5):
+    for k in range(5):
         scale_from(k)
 
-    def neighbours(i, carry):
+    def near_rows(i):
         for place in (1, 3):
             landed(xin.at[place, i], x_recv.at[place, i])
         for place in range(4):
             gather(sel[place + 1], xin[place, i], place + 2, i)
-        return carry
-
-    lax.fori_loop(0, tiles, neighbours, 0)
+
+    def own(i, carry):
+        for place in (0, 2):
+            landed(xin.at[place, i], x_recv.at[place, i])
+            fwd_copy(place, i).start()
+        landed(xmate.at[i], mate_recv.at[i])
+        gather(own_sel[0], xown[i], 0, i)
+        gather(own_sel[1], xmate[i], 1, i)
+
+        @pl.when(i > 0)
+        def _():
+            near_rows(i - 1)
+        return carry
+
+    lax.fori_loop(0, tiles, own, 0)
+    near_rows(tiles - 1)
     for k in range(5, 7):
         scale_from(k)
 
@@ -844,7 +850,7 @@
             i = 2 * half + c
             for e in range(local):
                 landed(ycross.at[half, e, pl.ds(lead, n_ep * cap - lead)], cross_recv.at[e, half])
-            for pos in range(2, n_ep):
+            for pos in (6, 7, 2, 3, 4, 5):
                 block_rows = slice(pos * cap, (pos + 1) * cap)
                 swapped = slice((pos ^ 1) * cap, ((pos ^ 1) + 1) * cap)
                 pieces = [rows_buf[e, block_rows, cols(i)] for e in range(local)] + [ycross[half, e, swapped, :] for e in range(local)]
@@ -864,16 +870,17 @@
                         cross_y(e, i).start()
                     ret[pl.ds(pl.multiple_of(3 * room + c * slab + e * cap, cap // 2), cap), cols(i)] = y[:cap]
                     mate_y(e, i).start()
-
-            @pl.when(half > 0)
-            def _():
-                finish_pair(half - 1)
+            finish_pair(half)
             return carry
 
         lax.fori_loop(0, tiles // 2, pair, 0)
-        finish_pair(tiles // 2 - 1)
 
     contract()
+
+    width = 3 * room + chip_slab
+    w_lane = lax.broadcasted_iota(jnp.int32, (tokens, width), 1).astype(f32)
+    for k in range(2):
+        comb[k * tokens:(k + 1) * tokens, :] = (w_lane == column_of(index[k])[:, 0:1]).astype(f32).astype(bf16)
 
     top = jnp.zeros((1, 1), f32)
     for s0, s1 in [(slots_row[0], slots_row[1])] + [(slots_in[k, 0:1, :], slots_in[k, 1:2, :]) for k in range(n_ep - 1)]:
@@ -904,7 +911,8 @@
         reps = tile // 128
         g0 = jnp.concatenate([gates[0]] * reps, axis=1)
         g1 = jnp.concatenate([gates[1]] * reps, axis=1)
-        out[:, cols(i)] = xown[i].astype(f32) + (g0 * picked[:tokens] + g1 * picked[tokens:])
+        done[i] = xown[i].astype(f32) + (g0 * picked[:tokens] + g1 * picked[tokens:])
+        pltpu.make_async_copy(done.at[i], out.at[:, cols(i)], out_sem.at[i]).start()
         return carry
 
     lax.fori_loop(0, tiles, finish, 0)
@@ -914,6 +922,7 @@
             landed(stage.at[0, 0], near_send.at[k, i])
         landed(stage.at[0, 0], far_send.at[i])
         landed(xown.at[0], mate_send.at[i])
+        pltpu.make_async_copy(done.at[i], out.at[:, cols(i)], out_sem.at[i]).wait()
         for k in range(3):
             landed(stage.at[0, 0], fwd_send.at[k, i])
         for e in range(local):
@@ -951,7 +960,7 @@
         functools.partial(packed_kernel, n_ep=n_ep, tile=tile, cap=cap, room=room),
         out_shape=(jax.ShapeDtypeStruct((tokens, d_model), jnp.float32), jax.ShapeDtypeStruct((1,), jnp.int32)),
         in_specs=[vmem] * 5 + [hbm] * 4,
-        out_specs=(vmem, pl.BlockSpec(memory_space=pltpu.SMEM)),
+        out_specs=(hbm, pl.BlockSpec(memory_space=pltpu.SMEM)),
         scratch_shapes=[
             pltpu.VMEM((2 * local, d_ff, d_model), bf16),
             pltpu.VMEM((4, d_ff, tile), bf16),
@@ -984,6 +993,7 @@
             dma((local, tiles // 2)), dma((local, tiles // 2)),
             dma((6, tiles // 2)), dma((3, tiles)),
             dma((n_ep - 1,)), dma((n_ep - 1,)),
+            pltpu.VMEM((tiles, tokens, tile), jnp.float32), dma((tiles,)),
         ],
         compiler_params=pltpu.CompilerParams(collective_id=1, has_side_effects=True, vmem_limit_bytes=VMEM_LIMIT),
         name="moe_packed",

time: 114 us -> 112 us (0.982)
    pallas_call x1, Pallas kernels: 80.5 us -> 79 us  [moe_packed(): pl.pallas_call(functools.partial(packed_kernel, n_ep=n_ep, tile=tile, cap...]
where the time goes in v3:
time: 112 us
  Pallas kernels  108 us (96%)
  other arithmetic  1.71 us (2%)
  between operations  1.38 us (1%)
    pallas_call x1, Pallas kernels, moe_packed(): pl.pallas_call(functools.partial(packed_kernel, n_ep=n_ep, tile=tile, cap...  79 us
    pallas_call x1, Pallas kernels, attention(): pl.pallas_call(functools.partial(attn_kernel, kv_heads=kv_heads, tile=til...  29 us

profile of v3, /device:TPU:81, one launch (start us, length us, event | category | flops | bytes accessed | tf_op | source)
XLA Modules:
  0.0 112.3 jit_solution(8184928554395071602)
XLA Ops:
  0.6 0.0 copy-start.1
  0.6 0.0 copy-start.2
  0.7 29.0 %attend.1 = (bf16[128,4096]{1,0:T(8,128)(2,1)}, bf16[128,32,8,128]{3,2,1,0:T(8,128)(2,1)}, bf16[128,32,8,128]{3,2,1,0:T(8,128)(2,1)}) custom-call(s32[128]{0:T(128)} %lens.1, bf16[128,4096]{1,0:T(8,128)(2,1)} %hidden.3, bf16[32,128]{1,0:T(8,128)(2,1)} %bitcast.21, s32[1,128]{1,0:T(1,128)} %bitcast.24, f32[1,128]{1,0:T(1,128)} %constant.5.clone.freq, ...), custom_call_target="tpu_custom_call" | custom-call | tf_op jit(solution)/shard_map/attend/pallas_call | solution.py:158
  29.7 0.0 copy-done.1
  29.7 0.0 copy-done.2
  29.7 79.0 %moe_packed.1 = (f32[128,4096]{1,0:T(8,128)}, s32[1]{0:T(128)}) custom-call(bf16[128,4096]{1,0:T(8,128)(2,1)} %get-tuple-element.47.mix, bf16[128,4096]{1,0:T(8,128)(2,1)} %hidden.3, s32[2,128]{1,0:T(2,128)S(1)} %bitcast.22, bf16[32,128]{1,0:T(8,128)(2,1)S(1)} %bitcast.19, bf16[16,4096]{1,0:T(8,128)(2,1)} %bitcast.17, bf16[4096,4096]{1,0:T(8,128)(2,1)} %wo.1, ...), custom_call_target="tpu_custom_call" | custom-call | tf_op jit(solution)/shard_map/moe_packed/pallas_call | solution.py:959
  109.4 1.9 %conditional.5 = (bf16[128,4096]{1,0:T(8,128)(2,1)S(1)}) conditional(s32[]{:T(128)} %bitcast.12, (s32[128,2]{0,1:T(2,128)S(1)}, bf16[4096]{0:T(1024)(128)(2,1)S(1)}, bf16[4096,16]{0,1:T(8,128)(2,1)}, bf16[2,4096,960]{1,2,0:T(8,128)(2,1)}, bf16[2,4096,960]{1,2,0:T(8,128)(2,1)}, /*index=5*/bf16[128,4096]{1,0:T(8,128)(2,1)}, ...), branch_computations={%region_0.0_spmd, %region_1.0_spmd} | conditional | flops 524288 | bytes 3145736
  109.6 1.7 %convert_element_type.15 = bf16[128,4096]{1,0:T(8,128)(2,1)S(1)} convert(f32[128,4096]{1,0:T(8,128)} %param.1) | non-fusion elementwise | flops 524288 | bytes 3145728 | tf_op jit(solution)/shard_map/cond/branch_0_fun/convert_element_type | solution.py:1016
  111.3 0.0 copy-start
  111.3 1.0 copy-done
Async XLA Ops:
  0.6 29.0 %copy-start.1 = (bf16[4096]{0:T(1024)(128)(2,1)S(1)}, bf16[4096]{0:T(1024)(128)(2,1)}, u32[]{:S(2)}) copy-start(bf16[4096]{0:T(1024)(128)(2,1)} %param.28) | copy-start | bytes 24580
  0.6 29.0 %copy-start.2 = (s32[128,2]{0,1:T(2,128)S(1)}, s32[128,2]{0,1:T(2,128)}, u32[]{:S(2)}) copy-start(s32[128,2]{0,1:T(2,128)} %param.22) | copy-start | bytes 3076
  111.3 1.0 copy-start
